TPU v7x, 32 devices: a whole 2x2x4 slice. The times are simulated.
32 devices in a mesh: row: 2 (over core), col: 4 (over y, x), depth: 4 (over z).
Axes of the slice: x: 2, y: 2, z: 4, core: 2. Of those that a mesh axis runs over, the one named last changes fastest.
Arguments:
- a_tile: float32 [2048, 2048], P('row', 'col'), as said below
- panels: float32 [2048, 4096], P('row', 'depth'), as said below
Outputs:
- trailing: float32 [2048, 2048], P(('row', 'depth'), 'col')
- new_panel: float32 [2048, 512], P(('row', 'col'))
- diag_norm: float32 [1], replicated
Inputs may be any that keep to these rules, and one draw needn't show every extreme that they name: symmetric; a_tile - panels panels^T is positive definite with a large positive diagonal. `panels`: real-valued entries of full rank.
All inputs are finite; a program needn't handle non-finite values.
Results may differ from a plain program's by a relative error of at most 0.00015.
Values sent between devices are 32-bit elements; how exact they have to be, the bound alone decides.
A program may use at most 64 MiB of HBM per device.

v0:
```python
import functools

import jax
import jax.numpy as jnp
from jax import lax
from jax.experimental import pallas as pl
from jax.experimental.pallas import tpu as pltpu
from jax.sharding import PartitionSpec as P

PB = 512
BLOCK = 128
NB = 32
CHUNK = 128
EARLY = 3
TILE = 256
HIGHEST = lax.Precision.HIGHEST
MESH = pl.DeviceIdType.MESH
F32 = jnp.float32
BF16 = jnp.bfloat16


def split(value):
    high = value.astype(BF16)
    return high, (value - high.astype(F32)).astype(BF16)


def dot_t(left, right):
    return lax.dot_general(left, right, (((1,), (1,)), ((), ())), preferred_element_type=F32)


def product(left_hi, left_lo, right_hi, right_lo):
    return dot_t(left_hi, right_hi) + (dot_t(left_hi, right_lo) + dot_t(left_lo, right_hi))


def mm(a, b, dims):
    return lax.dot_general(a, b, (dims, ((), ())), precision=HIGHEST, preferred_element_type=F32)


def factor_block(work, block, advance):
    work[:, :BLOCK] = block
    diag = lax.broadcasted_iota(jnp.int32, (BLOCK, BLOCK), 0) == lax.broadcasted_iota(jnp.int32, (BLOCK, BLOCK), 1)
    work[:, BLOCK:] = jnp.where(diag, 1.0, 0.0)
    sub = lax.broadcasted_iota(jnp.int32, (NB, BLOCK), 0)
    for j in range(0, BLOCK, NB):
        left = work[j:j + NB, :BLOCK]
        right = work[j:j + NB, BLOCK:]
        advance()
        lanes = [jnp.broadcast_to(left[:, j + k:j + k + 1], (NB, BLOCK)) for k in range(NB)]
        for k in range(NB):
            inv = lax.rsqrt(lanes[k][k:k + 1])
            col = lanes[k] * inv
            for i in range(k + 1, NB):
                lanes[i] = lanes[i] - col * col[i:i + 1]
            row_l = left[k:k + 1] * inv
            row_r = right[k:k + 1] * inv
            below = jnp.where(sub > k, col, 0.0)
            left = jnp.where(sub == k, row_l, left - below * row_l)
            right = jnp.where(sub == k, row_r, right - below * row_r)
        work[j:j + NB, :BLOCK] = left
        work[j:j + NB, BLOCK:] = right
        if j + NB < BLOCK:
            both = jnp.concatenate([left, right], axis=1)
            work[j + NB:, :] = work[j + NB:, :] - mm(left[:, j + NB:], both, ((0,), (0,)))
    return work[:, BLOCK:]


def gather_update(sizes, split_d, a_ref, p_ref, out_ref, x_ref, n_ref, *scratch):
    nr, nc, nd = sizes
    (own_hi, own_lo, oth_hi, oth_lo, p0, pc, part, up, down, cpart, crecv, arow, nbuf, psum,
     pair_send, pair_recv, a_send, a_recv, rs_send, rs_recv, ag_send, ag_recv, d_send, d_recv,
     f_send, f_recv, up_send, up_recv, down_send, down_recv, n_send, n_recv,
     c_ref, d_ref, work, invs, fact, rest, dpart, drecv, adiag, ds_send, ds_recv, da_send, da_recv, ad_send, ad_recv) = scratch
    tile_rows, tile_cols = a_ref.shape
    share = tile_rows // nd
    crows = tile_rows // nc
    piece = crows // nd
    slab = PB // nc
    d_high, d_wide = split_d
    r, c, z = lax.axis_index("row"), lax.axis_index("col"), lax.axis_index("depth")
    chunks = tile_cols // CHUNK

    def at(row, col, depth):
        return (row, col, depth)

    def remote(src, dst, send, recv, device):
        return pltpu.make_async_remote_copy(
            src_ref=src, dst_ref=dst, send_sem=send, recv_sem=recv, device_id=device, device_id_type=MESH)

    def rows(start, size):
        return pl.ds(pl.multiple_of(start, size), size)

    barrier = pltpu.get_barrier_semaphore()
    for k in range(1, nd):
        pl.semaphore_signal(barrier, inc=1, device_id=at(r, c, lax.rem(z + k, nd)), device_id_type=MESH)
    for m in range(1, nc):
        pl.semaphore_signal(barrier, inc=1, device_id=at(r, lax.rem(c + m, nc), z), device_id_type=MESH)
    pl.semaphore_signal(barrier, inc=1, device_id=at(1 - r, c, z), device_id_type=MESH)

    def split_own(t):
        hi, lo = split(p_ref[rows(t * TILE, TILE), :])
        own_hi[rows(t * TILE, TILE), :] = hi
        own_lo[rows(t * TILE, TILE), :] = lo

    pl.loop(0, PB // TILE)(split_own)
    pl.semaphore_wait(barrier, nd - 1 + nc - 1 + 1)

    partner = at(1 - r, c, z)
    first = c * tile_cols
    owner = first // tile_rows
    offset = lax.rem(first, tile_rows)
    head_copy = remote(p_ref.at[pl.ds(0, PB), :], p0, pair_send.at[0], pair_recv.at[0], partner)
    col_copy = remote(p_ref.at[rows(offset, tile_cols), :], pc, pair_send.at[1], pair_recv.at[1], partner)

    def a_copy(m):
        to = lax.rem(c + m, nc)
        return remote(a_ref.at[rows(to * crows + z * piece, piece), pl.ds(0, PB)], arow,
                      a_send.at[m], a_recv, at(r, to, z))

    def patch(depth):
        return (rows(depth // (PB // d_wide) * d_high, d_high),
                rows(lax.rem(depth, PB // d_wide) * d_wide, d_wide))

    def in_slab(col, depth):
        high, wide = patch(depth)
        return (rows(col * slab + depth // (PB // d_wide) * d_high, d_high), wide)

    def ad_copy(m):
        to = lax.rem(c + m, nc)
        return remote(a_ref.at[in_slab(to, z)], adiag, ad_send.at[m], ad_recv, at(r, to, z))

    def ds_copy(k):
        to = lax.rem(z + k, nd)
        return remote(dpart.at[patch(to)], drecv.at[k], ds_send.at[k], ds_recv.at[k], at(r, c, to))

    def da_copy(k):
        here = d_ref.at[in_slab(c, z)]
        return remote(here, here, da_send.at[k], da_recv.at[k], at(r, c, lax.rem(z + k, nd)))

    def da_from(k):
        there = d_ref.at[in_slab(c, lax.rem(z - k + nd, nd))]
        return remote(there, there, da_send.at[k], da_recv.at[k], at(r, c, lax.rem(z + k, nd)))

    @pl.when(r == 0)
    def _():
        head_copy.start()

        @pl.when(c == 0)
        def _():
            for m in range(1, nc):
                ad_copy(m).start()

    @pl.when(c == 0)
    def _():
        for m in range(1, nc):
            a_copy(m).start()

    @pl.when(r == owner)
    def _():
        col_copy.start()

    @pl.when(r == 0)
    def _():
        oth_hi[...] = own_hi[pl.ds(0, PB), :]
        oth_lo[...] = own_lo[pl.ds(0, PB), :]
        band = rows(c * slab, slab)
        dpart[...] = product(own_hi[band, :], own_lo[band, :], oth_hi[...], oth_lo[...])
        for k in range(1, nd):
            ds_copy(k).start()

    pl.loop(PB // TILE, tile_rows // TILE)(split_own)

    @pl.when(r != 0)
    def _():
        head_copy.wait_recv()
        hi, lo = split(p0[...])
        oth_hi[...] = hi
        oth_lo[...] = lo

    mine = rows(c * crows, crows)
    cpart[...] = product(own_hi[mine, :], own_lo[mine, :], oth_hi[...], oth_lo[...])

    def rs_copy(k):
        to = lax.rem(z + k, nd)
        return remote(cpart.at[rows(to * piece, piece), :], crecv.at[k], rs_send.at[k], rs_recv.at[k], at(r, c, to))

    for k in range(1, nd):
        rs_copy(k).start()

    @pl.when(r == 0)
    def _():
        @pl.when(c == 0)
        def _():
            adiag[...] = a_ref[in_slab(0, z)]

        @pl.when(c != 0)
        def _():
            ad_copy(1).wait_recv()

        dsum = dpart[patch(z)]
        for k in range(1, nd):
            ds_copy(k).wait_recv()
            dsum = dsum + drecv[k]
        d_ref[in_slab(c, z)] = adiag[...] - dsum
        for k in range(1, nd):
            da_copy(k).start()

    @pl.when(r == owner)
    def _():
        oth_hi[...] = own_hi[rows(offset, tile_cols), :]
        oth_lo[...] = own_lo[rows(offset, tile_cols), :]

    @pl.when(r != owner)
    def _():
        col_copy.wait_recv()
        hi, lo = split(pc[...])
        oth_hi[...] = hi
        oth_lo[...] = lo

    @pl.loop(0, tile_rows // TILE)
    def _(t):
        at_rows = rows(t * TILE, TILE)
        part[at_rows, :] = product(own_hi[at_rows, :], own_lo[at_rows, :], oth_hi[...], oth_lo[...])

    def d_piece(col, k):
        return d_ref.at[in_slab(col, lax.rem(z - k + nd, nd))]

    def d_copy(k, m):
        return remote(d_piece(c, k), d_piece(c, k), d_send.at[k, m], d_recv.at[k, m], at(r, lax.rem(c + m, nc), z))

    def d_from(k, m):
        there = d_piece(lax.rem(c - m + nc, nc), k)
        return remote(there, there, d_send.at[k, m], d_recv.at[k, m], at(r, lax.rem(c + m, nc), z))

    def f_copy(k, m):
        there = d_piece(lax.rem(c - m + nc, nc), k)
        return remote(there, there, f_send.at[k, m], f_recv.at[k, m], partner)

    @pl.when(r == 0)
    def _():
        for k in range(nd):
            if k:
                da_from(k).wait_recv()
            for m in range(1, nc):
                d_copy(k, m).start()
            f_copy(k, 0).start()

    @pl.when(c == 0)
    def _():
        arow[...] = a_ref[rows(z * piece, piece), pl.ds(0, PB)]

    @pl.when(c != 0)
    def _():
        a_copy(1).wait_recv()

    total = cpart[rows(z * piece, piece), :]
    for k in range(1, nd):
        rs_copy(k).wait_recv()
        total = total + crecv[k]
    c_ref[rows(z * piece, piece), :] = arow[...] - total

    def ag_copy(k):
        here = rows(z * piece, piece)
        return remote(c_ref.at[here, :], c_ref.at[here, :], ag_send.at[k], ag_recv.at[k],
                      at(r, c, lax.rem(z + k, nd)))

    def ag_from(k):
        there = rows(lax.rem(z - k + nd, nd) * piece, piece)
        return remote(c_ref.at[there, :], c_ref.at[there, :], ag_send.at[k], ag_recv.at[k], at(r, c, lax.rem(z + k, nd)))

    for k in range(1, nd):
        ag_copy(k).start()

    def up_copy(b, ch):
        lanes = rows(ch * CHUNK, CHUNK)
        return remote(part.at[rows(b * share, share), lanes], up.at[rows(b * share, share), lanes],
                      up_send.at[b, ch], up_recv.at[b, ch], at(r, c, lax.rem(z + 1, nd)))

    def down_copy(b, ch):
        lanes = rows(ch * CHUNK, CHUNK)
        return remote(part.at[rows(b * share, share), lanes], down.at[rows(b * share, share), lanes],
                      down_send.at[b, ch], down_recv.at[b, ch], at(r, c, lax.rem(z + nd - 1, nd)))

    def tick(i):
        u = i - z
        @pl.when(jnp.logical_and(u >= 0, u < (nd - z) * chunks))
        def _():
            b = nd - 1 - u // chunks
            ch = lax.rem(u, chunks)
            here = (rows(b * share, share), rows(ch * CHUNK, CHUNK))

            @pl.when(z > 0)
            def _():
                up_copy(b, ch).wait_recv()
                part[here] = part[here] + up[here]

            @pl.when(b > z)
            def _():
                up_copy(b, ch).start()

        v = i - (nd - 1 - z)
        @pl.when(jnp.logical_and(v >= 0, v < (z + 1) * chunks))
        def _():
            b = v // chunks
            ch = lax.rem(v, chunks)
            here = (rows(b * share, share), rows(ch * CHUNK, CHUNK))

            @pl.when(z < nd - 1)
            def _():
                down_copy(b, ch).wait_recv()
                part[here] = part[here] + down[here]

            @pl.when(b < z)
            def _():
                down_copy(b, ch).start()

    ticks = nd * chunks + nd - 1
    slots = PB // NB + EARLY
    done = []

    def advance(last=False):
        first_tick = len(done) * ticks // slots
        done.append(None)
        pl.loop(first_tick, ticks if last else min(ticks, len(done) * ticks // slots))(tick)

    for _ in range(EARLY):
        advance()

    @pl.when(r == 0)
    def _():
        for k in range(nd):
            for m in range(1, nc):
                d_from(k, m).wait_recv()
                f_copy(k, m).start()

    @pl.when(r != 0)
    def _():
        for k in range(nd):
            for m in range(nc):
                f_copy(k, m).wait_recv()

    for s in range(0, PB, BLOCK):
        e = s + BLOCK
        inv = factor_block(work, (fact if s else d_ref)[s:e, s:e], advance)
        invs[s // BLOCK] = inv
        if e < PB:
            u = mm(inv, (fact if s else d_ref)[s:e, e:], ((1,), (0,)))
            fact[s:e, e:] = u
            fact[e:, e:] = (fact if s else d_ref)[e:, e:] - mm(u, u, ((0,), (0,)))

    for k in range(1, nd):
        ag_from(k).wait_recv()
    rest[...] = c_ref[...]
    for s in range(0, PB, BLOCK):
        e = s + BLOCK
        x = mm(rest[:, s:e], invs[s // BLOCK], ((1,), (1,)))
        x_ref[:, s:e] = x
        if e < PB:
            rest[:, e:] = rest[:, e:] - mm(x, fact[s:e, e:], ((1,), (0,)))

    trailing = a_ref[rows(z * share, share), :] - part[rows(z * share, share), :]
    out_ref[...] = trailing
    grow = r * tile_rows + z * share + lax.broadcasted_iota(jnp.int32, trailing.shape, 0)
    gcol = first + lax.broadcasted_iota(jnp.int32, trailing.shape, 1)
    squares = jnp.where(grow == gcol, trailing * trailing, 0.0)
    acc = squares.reshape(share // 8, 8, tile_cols).sum(0)
    acc = acc.reshape(8, chunks, CHUNK).sum(1) if chunks == 1 else sum(
        acc[:, i * CHUNK:(i + 1) * CHUNK] for i in range(chunks))
    psum[0] = acc

    stages = ((nd, lambda k: at(r, c, lax.rem(z + k, nd))), (nc, lambda k: at(r, lax.rem(c + k, nc), z)),
              (nr, lambda k: partner))
    base = 0
    for stage, (count, peer) in enumerate(stages):
        def n_copy(k):
            return remote(psum.at[stage], nbuf.at[base + k], n_send.at[base + k], n_recv.at[base + k], peer(k))
        for k in range(1, count):
            n_copy(k).start()
        for k in range(1, count):
            n_copy(k).wait_recv()
            acc = acc + nbuf[base + k]
        psum[stage + 1] = acc
        for k in range(1, count):
            n_copy(k).wait_send()
        base += count
    n_ref[...] = jnp.sqrt(jnp.sum(acc, keepdims=True) / (tile_cols * nc))

    @pl.when(r == 0)
    def _():
        head_copy.wait_send()

        @pl.when(c == 0)
        def _():
            for m in range(1, nc):
                ad_copy(m).wait_send()

        for k in range(nd):
            for m in range(nc):
                f_copy(k, m).wait_send()
                if m:
                    d_copy(k, m).wait_send()
            if k:
                ds_copy(k).wait_send()
                da_copy(k).wait_send()

    @pl.when(r == owner)
    def _():
        col_copy.wait_send()

    @pl.when(c == 0)
    def _():
        for m in range(1, nc):
            a_copy(m).wait_send()

    for k in range(1, nd):
        rs_copy(k).wait_send()
        ag_copy(k).wait_send()

    @pl.loop(0, nd)
    def _(b):
        for ch in range(chunks):
            @pl.when(b > z)
            def _():
                up_copy(b, ch).wait_send()

            @pl.when(b < z)
            def _():
                down_copy(b, ch).wait_send()


def local(sizes, a_tile, panels):
    nr, nc, nd = sizes
    tile_rows, tile_cols = a_tile.shape
    k_size = panels.shape[1]
    share, crows = tile_rows // nd, tile_rows // nc
    piece, chunks, slab = crows // nd, tile_cols // CHUNK, PB // nc
    high = max(8, slab // nd)
    split_d = (high, slab * PB // (nd * high))
    vmem = pl.BlockSpec(memory_space=pltpu.VMEM)
    shape = lambda *s: jax.ShapeDtypeStruct(s, F32)
    dma = lambda *s: pltpu.SemaphoreType.DMA(s)
    wide = max(PB, tile_cols)
    trailing, new_panel, norm = pl.pallas_call(
        functools.partial(gather_update, sizes, split_d),
        out_shape=(shape(share, tile_cols), shape(crows, PB), shape(1, 1)),
        in_specs=[vmem] * 2,
        out_specs=(vmem,) * 3,
        scratch_shapes=[
            pltpu.VMEM((tile_rows, k_size), BF16), pltpu.VMEM((tile_rows, k_size), BF16),
            pltpu.VMEM((wide, k_size), BF16), pltpu.VMEM((wide, k_size), BF16),
            pltpu.VMEM((PB, k_size), F32), pltpu.VMEM((tile_cols, k_size), F32),
            pltpu.VMEM((tile_rows, tile_cols), F32), pltpu.VMEM((tile_rows, tile_cols), F32),
            pltpu.VMEM((tile_rows, tile_cols), F32), pltpu.VMEM((crows, PB), F32),
            pltpu.VMEM((nd, piece, PB), F32), pltpu.VMEM((piece, PB), F32),
            pltpu.VMEM((nr + nc + nd, 8, CHUNK), F32), pltpu.VMEM((4, 8, CHUNK), F32),
            dma(2), dma(2), dma(nc), pltpu.SemaphoreType.DMA, dma(nd), dma(nd), dma(nd), dma(nd),
            dma(nd, nc), dma(nd, nc), dma(nd, nc), dma(nd, nc),
            dma(nd, chunks), dma(nd, chunks), dma(nd, chunks), dma(nd, chunks),
            dma(nr + nc + nd), dma(nr + nc + nd),
            pltpu.VMEM((crows, PB), F32), pltpu.VMEM((PB, PB), F32), pltpu.VMEM((BLOCK, 2 * BLOCK), F32),
            pltpu.VMEM((PB // BLOCK, BLOCK, BLOCK), F32), pltpu.VMEM((PB, PB), F32), pltpu.VMEM((crows, PB), F32),
            pltpu.VMEM((slab, PB), F32), pltpu.VMEM((nd, *split_d), F32), pltpu.VMEM(split_d, F32),
            dma(nd), dma(nd), dma(nd), dma(nd), dma(nc), pltpu.SemaphoreType.DMA,
        ],
        compiler_params=pltpu.CompilerParams(collective_id=0, has_side_effects=True, vmem_limit_bytes=60 << 20),
        name="gather_update",
    )(a_tile, panels)
    return (trailing, new_panel, norm.reshape(1))


def solution(mesh):
    sizes = tuple(mesh.shape[axis] for axis in ("row", "col", "depth"))
    return jax.shard_map(
        functools.partial(local, sizes),
        mesh=mesh,
        in_specs=(P("row", "col"), P("row", "depth")),
        out_specs=(P(("row", "depth"), "col"), P(("row", "col"), None), P()),
        check_vma=False,
    )
```

profile of v0, /device:TPU:0, one launch (start us, length us, event | category | flops | bytes accessed | tf_op | source)
XLA Modules:
  0.0 107.1 jit_solution(18383677319006580729)
XLA Ops:
  0.6 101.0 %gather_update.1 = (f32[256,512]{1,0:T(8,128)}, f32[256,512]{1,0:T(8,128)}, f32[1,1]{1,0:T(1,128)}) custom-call(f32[1024,512]{1,0:T(8,128)} %a_ref.1, f32[1024,1024]{1,0:T(8,128)} %p_ref.1), custom_call_target="tpu_custom_call" | custom-call | tf_op jit(solution)/shard_map/gather_update/pallas_call | solution.py:442
  101.7 1.9 %copy.8 = f32[256,512]{1,0:T(8,128)} copy(f32[256,512]{1,0:T(8,128)} %get-tuple-element.12) | data formatting | bytes 1048576
  103.5 1.9 %copy.9 = f32[256,512]{1,0:T(8,128)} copy(f32[256,512]{1,0:T(8,128)} %get-tuple-element.13) | data formatting | bytes 1048576
where the time goes:
time: 107 us
  Pallas kernels  101 us (94%)
  local copies, waits for them, and re-layouts  3.74 us (3%)
  between operations  2.33 us (2%)
    pallas_call x1, Pallas kernels, local(): pl.pallas_call(functools.partial(gather_update, sizes, split_d), out_shap...  101 us
    unnamed x2, local copies, waits for them, and re-layouts  3.74 us

commit v1 on v0

v1 whole, which is shorter than its diff:
```python
import functools

import jax
import jax.numpy as jnp
from jax import lax
from jax.experimental import pallas as pl
from jax.experimental.pallas import tpu as pltpu
from jax.sharding import PartitionSpec as P

PB = 512
BLOCK = 128
NB = 32
LANES = 128
TILE = 256
EVENTS = {"open": 20.0, "tick": 1.15, "first": 13.0, "step": 2.8, "hop": 4.5}
HIGHEST = lax.Precision.HIGHEST
MESH = pl.DeviceIdType.MESH
F32 = jnp.float32
BF16 = jnp.bfloat16


def split(value):
    high = value.astype(BF16)
    return high, (value - high.astype(F32)).astype(BF16)


def dot_t(left, right):
    return lax.dot_general(left, right, (((1,), (1,)), ((), ())), preferred_element_type=F32)


def product(left_hi, left_lo, right_hi, right_lo):
    return dot_t(left_hi, right_hi) + (dot_t(left_hi, right_lo) + dot_t(left_lo, right_hi))


def mm(a, b, dims):
    return lax.dot_general(a, b, (dims, ((), ())), precision=HIGHEST, preferred_element_type=F32)


def factor_block(work, block, advance):
    work[:, :BLOCK] = block
    diag = lax.broadcasted_iota(jnp.int32, (BLOCK, BLOCK), 0) == lax.broadcasted_iota(jnp.int32, (BLOCK, BLOCK), 1)
    work[:, BLOCK:] = jnp.where(diag, 1.0, 0.0)
    sub = lax.broadcasted_iota(jnp.int32, (NB, BLOCK), 0)
    for j in range(0, BLOCK, NB):
        left = work[j:j + NB, :BLOCK]
        right = work[j:j + NB, BLOCK:]
        advance()
        lanes = [jnp.broadcast_to(left[:, j + k:j + k + 1], (NB, BLOCK)) for k in range(NB)]
        for k in range(NB):
            inv = lax.rsqrt(lanes[k][k:k + 1])
            col = lanes[k] * inv
            for i in range(k + 1, NB):
                lanes[i] = lanes[i] - col * col[i:i + 1]
            row_l = left[k:k + 1] * inv
            row_r = right[k:k + 1] * inv
            below = jnp.where(sub > k, col, 0.0)
            left = jnp.where(sub == k, row_l, left - below * row_l)
            right = jnp.where(sub == k, row_r, right - below * row_r)
        work[j:j + NB, :BLOCK] = left
        work[j:j + NB, BLOCK:] = right
        if j + NB < BLOCK:
            both = jnp.concatenate([left, right], axis=1)
            work[j + NB:, :] = work[j + NB:, :] - mm(left[:, j + NB:], both, ((0,), (0,)))
    return work[:, BLOCK:]


def plan(nr, nc, heads):
    lists = [[] for _ in range(nr * nc)]
    for g in range(heads, nr * nc):
        lists[g] = [(g, j) for j in range(heads)] + [(g, g)]
    for low in range(heads, nr * nc):
        for high in range(low + 1, nr * nc):
            able = [g for g in range(nr * nc) if g < nc or g // nc == low // nc]
            best = min(able, key=lambda g: (len(lists[g]), g not in (low, high), g))
            lists[best].append((low, high) if best == low else (high, low))
    return lists


def kernel(sizes, lists, a_ref, p_ref, out_ref, x_ref, n_ref, *scratch):
    nr, nc, nd = sizes
    (hi, lo, oth, part, rin, fin, turned, tin, dpart, drin, d_ref, adbuf, acbuf, psum, nbuf,
     work, invs, fact, rest,
     pair_send, pair_recv, ad_send, ad_recv, ac_send, ac_recv, in_send, in_recv, out_send, out_recv,
     di_send, di_recv, do_send, do_recv, d_send, d_recv, f_send, f_recv, t_send, t_recv, n_send, n_recv) = scratch
    tile_rows, tile_cols = a_ref.shape
    size = tile_rows // nc
    half = size // 2
    heads = PB // size
    wide = tile_cols // size
    share = tile_rows // nd
    sub = BLOCK // nc
    steps = PB // BLOCK
    slots = max(map(len, lists))
    devices = nr * nc * nd
    r, c, z = lax.axis_index("row"), lax.axis_index("col"), lax.axis_index("depth")
    g = r * nc + c
    mid = nd // 2
    low = z < mid
    center = jnp.logical_or(z == mid - 1, z == mid)
    edge = jnp.logical_or(z == 0, z == nd - 1)
    inner = jnp.logical_not(edge)
    side = jnp.where(center, 1, 0)
    inward = jnp.where(low, z + 1, z - 1)
    outward = jnp.where(low, z - 1, z + 1)
    zb = z * share // size
    zo = lax.rem(z * share, size)
    first, second = r == 0, r != 0
    partner = (1 - r, c, z)
    both = jnp.logical_and

    def pick(values):
        result = jnp.int32(values[0])
        for i, value in enumerate(values[1:], 1):
            result = jnp.where(g == i, value, result)
        return result

    xs = [pick([l[s][0] if s < len(l) else 0 for l in lists]) for s in range(slots)]
    ys = [pick([l[s][1] if s < len(l) else 0 for l in lists]) for s in range(slots)]
    counts = pick([len(l) for l in lists])
    valid = [s < counts for s in range(slots)]
    near = [both(valid[s], both(xs[s] // nc == r, ys[s] // nc == r)) for s in range(slots)]
    far = [both(valid[s], jnp.logical_not(both(xs[s] // nc == r, ys[s] // nc == r))) for s in range(slots)]

    def remote(src, dst, send, recv, device):
        return pltpu.make_async_remote_copy(
            src_ref=src, dst_ref=dst, send_sem=send, recv_sem=recv, device_id=device, device_id_type=MESH)

    def rows(start, count):
        return pl.ds(pl.multiple_of(start, count), count)

    barrier = pltpu.get_barrier_semaphore()
    me = g * nd + z

    def device(i):
        there = lax.rem(me + i, devices)
        return (there // (nc * nd), lax.rem(there // nd, nc), lax.rem(there, nd))

    @pl.loop(1, devices)
    def _(i):
        pl.semaphore_signal(barrier, inc=1, device_id=device(i), device_id_type=MESH)

    @pl.loop(0, tile_rows // TILE)
    def _(t):
        high, rem = split(p_ref[rows(t * TILE, TILE), :])
        here = rows(r * tile_rows + t * TILE, TILE)
        hi[here, :] = high
        lo[here, :] = rem

    def compute(s):
        a, b = rows(xs[s] * size, size), rows(ys[s] * size, size)
        part[s] = -product(hi[a, :], lo[a, :], hi[b, :], lo[b, :])

    @pl.when(first)
    def _():
        at = [pl.ds(pl.multiple_of(k * BLOCK + c * sub, sub), sub) for k in range(steps)]
        left_hi = jnp.concatenate([hi[i, :] for i in at], axis=0)
        left_lo = jnp.concatenate([lo[i, :] for i in at], axis=0)
        dpart[...] = -product(left_hi, left_lo, hi[:PB, :], lo[:PB, :])

    for s in range(slots):
        pl.when(near[s])(functools.partial(compute, s))

    pl.semaphore_wait(barrier, devices - 1)

    def pair_copy(j):
        return remote(p_ref.at[rows(j * size, size), :], oth.at[j], pair_send.at[j], pair_recv.at[j], partner)

    def d_fold(k):
        return mid - 1 + k % 2

    def c_fold(q):
        return (mid - 1, mid, 0, nd - 1)[q % 4]

    def d_at(col, k):
        return (pl.ds(pl.multiple_of(k * BLOCK + col * sub, sub), sub), pl.ds(k * BLOCK, PB - k * BLOCK))

    def d_in(k):
        return (pl.ds(k * sub, sub), pl.ds(k * BLOCK, PB - k * BLOCK))

    def ad_copy(k, to):
        return remote(a_ref.at[d_at(to, k)], adbuf.at[d_in(k)], ad_send.at[k, to], ad_recv.at[k], (r, to, z))

    def ac_at(col, q):
        return (rows(col * size + q % 2 * half, half), pl.ds(q // 2 * size, size))

    def ac_copy(q, to):
        return remote(a_ref.at[ac_at(to, q)], acbuf.at[q], ac_send.at[q, to], ac_recv.at[q], (r, to, z))

    @pl.when(first)
    def _():
        for j in range(heads):
            pair_copy(j).start()

    @pl.when(second)
    def _():
        for j in range(nc):
            pair_copy(j).start()

    def folds(act):
        @pl.when(c == 0)
        def _():
            for k in range(steps):
                @pl.when(both(first, z == d_fold(k)))
                def _():
                    for to in range(1, nc):
                        act(ad_copy(k, to))
            for q in range(2 * heads):
                for to in range(1, nc):
                    @pl.when(both(z == c_fold(q), r * nc + to >= heads))
                    def _():
                        act(ac_copy(q, to))

    folds(lambda copy: copy.start())

    def din_copy(k):
        return remote(dpart.at[d_in(k)], drin.at[(side,) + d_in(k)], di_send.at[k], di_recv.at[side, k], (r, c, inward))

    def din_wait(at, k):
        here = drin.at[(at,) + d_in(k)]
        remote(here, here, di_send.at[k], di_recv.at[at, k], (r, c, inward)).wait_recv()
        return here

    def stage_d(k):
        @pl.when(inner)
        def _():
            dpart[d_in(k)] = dpart[d_in(k)] + din_wait(0, k)[...]

        @pl.when(z == d_fold(k))
        def _():
            @pl.when(c == 0)
            def _():
                dpart[d_in(k)] = dpart[d_in(k)] + a_ref[d_at(0, k)]

            @pl.when(c != 0)
            def _():
                ad_copy(k, 1).wait_recv()
                dpart[d_in(k)] = dpart[d_in(k)] + adbuf[d_in(k)]

        din_copy(k).start()

    def dout_copy(k):
        here = d_ref.at[d_at(c, k)]
        return remote(here, here, do_send.at[k], do_recv.at[k], (r, c, outward))

    def d_copy(k, m):
        here = d_ref.at[d_at(c, k)]
        return remote(here, here, d_send.at[k, m], d_recv.at[k, m], (r, lax.rem(c + m, nc), z))

    def d_from(k, m):
        there = d_ref.at[d_at(lax.rem(c - m + nc, nc), k)]
        return remote(there, there, d_send.at[k, m], d_recv.at[k, m], (r, lax.rem(c + m, nc), z))

    def f_copy(k, m):
        there = d_ref.at[d_at(lax.rem(c - m + nc, nc), k)]
        return remote(there, there, f_send.at[k, m], f_recv.at[k, m], partner)

    def spread_d(k):
        @pl.when(inner)
        def _():
            dout_copy(k).start()

        for m in range(1, nc):
            d_copy(k, m).start()
        f_copy(k, 0).start()

    def chunk(q):
        return (q // 2, pl.ds(q % 2 * half, half), slice(None))

    def in_copy(q):
        return remote(part.at[chunk(q)], rin.at[(side,) + chunk(q)], in_send.at[q], in_recv.at[side, q], (r, c, inward))

    def in_wait(at, q):
        here = rin.at[(at,) + chunk(q)]
        remote(here, here, in_send.at[q], in_recv.at[at, q], (r, c, inward)).wait_recv()
        return here

    def out_copy(q):
        here = fin.at[chunk(q)]
        return remote(here, here, out_send.at[q], out_recv.at[q], (r, c, outward))

    def stage_a(q):
        @pl.when(inner)
        def _():
            part[chunk(q)] = part[chunk(q)] + in_wait(0, q)[...]

        if q < 2 * heads:
            @pl.when(both(g >= heads, z == c_fold(q)))
            def _():
                @pl.when(c == 0)
                def _():
                    part[chunk(q)] = part[chunk(q)] + a_ref[ac_at(0, q)]

                @pl.when(c != 0)
                def _():
                    ac_copy(q, 1).wait_recv()
                    part[chunk(q)] = part[chunk(q)] + acbuf[q]

        in_copy(q).start()

    def here_is(device):
        return both(device[0] == r, device[1] == c)

    def routes(s):
        x, y = xs[s], ys[s]
        straight = (x // nc, y // wide, z)
        across = (y // nc, x // wide, z)
        return (
            (both(valid[s], zb == lax.rem(x, nc)), fin.at[s, rows(zo, share), :], lax.rem(y, wide), straight),
            (both(both(valid[s], x != y), zb == lax.rem(y, nc)), turned.at[s, rows(zo, share), :], lax.rem(x, wide), across),
        )

    def deliver(s):
        for way, (cond, src, spot, to) in enumerate(routes(s)):
            @pl.when(cond)
            def _():
                if way:
                    turned[s] = fin[s].T

                @pl.when(here_is(to))
                def _():
                    pltpu.make_async_copy(src, tin.at[spot], t_recv.at[spot]).start()

                @pl.when(jnp.logical_not(here_is(to)))
                def _():
                    remote(src, tin.at[spot], t_send.at[s, way], t_recv.at[spot], to).start()

    def stage_b(q):
        @pl.when(both(valid[q // 2], center))
        def _():
            fin[chunk(q)] = part[chunk(q)] + in_wait(1, q)[...]

            @pl.when(inner)
            def _():
                out_copy(q).start()

            if q % 2:
                deliver(q // 2)

    def stage_c(q):
        @pl.when(both(valid[q // 2], jnp.logical_not(center)))
        def _():
            out_copy(q).wait_recv()

            @pl.when(inner)
            def _():
                out_copy(q).start()

            if q % 2:
                deliver(q // 2)

    def inner_a(q):
        pl.when(both(valid[q // 2], inner))(functools.partial(stage_a, q))

    def edge_a(s, cond):
        @pl.when(both(edge, cond))
        def _():
            stage_a(2 * s)
            stage_a(2 * s + 1)

    @pl.when(both(first, edge))
    def _():
        for k in range(steps):
            stage_d(k)

    for s in range(slots):
        edge_a(s, both(first, near[s]))

    @pl.when(second)
    def _():
        for j in range(heads):
            pair_copy(j).wait_recv()
            high, rem = split(oth[j])
            hi[pl.ds(j * size, size), :] = high
            lo[pl.ds(j * size, size), :] = rem
        for s in range(heads):
            compute(s)

    for s in range(slots):
        edge_a(s, both(second, valid[s]))

    @pl.when(both(first, inner))
    def _():
        for k in range(steps):
            stage_d(k)

    def center_d(k):
        d_ref[d_at(c, k)] = dpart[d_in(k)] + din_wait(1, k)[...]
        spread_d(k)

    @pl.when(both(first, center))
    def _():
        for k in range(steps):
            center_d(k)

    @pl.when(first)
    def _():
        for j in range(nc):
            pair_copy(j).wait_recv()
            high, rem = split(oth[j])
            here = pl.ds(tile_rows + j * size, size)
            hi[here, :] = high
            lo[here, :] = rem
        for s in range(slots):
            pl.when(far[s])(functools.partial(compute, s))

    for s in range(slots):
        edge_a(s, both(first, far[s]))

    times = EVENTS
    events = []
    for q in range(2 * slots):
        t = times["first"] + times["step"] * q
        events.append((t, functools.partial(inner_a, q)))
        events.append((t + times["hop"], functools.partial(stage_b, q)))
        events.append((t + 2 * times["hop"], functools.partial(stage_c, q)))
    events.sort(key=lambda e: e[0])
    clock = [times["open"]]

    def advance(amount=0):
        while events and events[0][0] <= clock[0]:
            events.pop(0)[1]()
        clock[0] += amount

    @pl.when(both(first, jnp.logical_not(center)))
    def _():
        for k in range(steps):
            dout_copy(k).wait_recv()
            spread_d(k)

    @pl.when(first)
    def _():
        for k in range(steps):
            for m in range(1, nc):
                d_from(k, m).wait_recv()
                f_copy(k, m).start()

    @pl.when(second)
    def _():
        for k in range(steps):
            for m in range(nc):
                f_copy(k, m).wait_recv()

    for s in range(0, PB, BLOCK):
        e = s + BLOCK
        src = fact if s else d_ref
        inv = factor_block(work, src[s:e, s:e], lambda: advance(times["tick"]))
        invs[s // BLOCK] = inv
        if e < PB:
            u = mm(inv, src[s:e, e:], ((1,), (0,)))
            fact[s:e, e:] = u
            for j in range(e, PB, BLOCK):
                fact[j:j + BLOCK, j:] = src[j:j + BLOCK, j:] - mm(u[:, j - e:j - e + BLOCK], u[:, j - e:], ((0,), (0,)))

    @pl.when(both(first, c < heads))
    def _():
        for i in range(1, steps):
            for j in range(i):
                d_ref[i * BLOCK:(i + 1) * BLOCK, j * BLOCK:(j + 1) * BLOCK] = (
                    d_ref[j * BLOCK:(j + 1) * BLOCK, i * BLOCK:(i + 1) * BLOCK].T)

    while any(event.args[0] < 2 * heads for _, event in events):
        events.pop(0)[1]()

    @pl.when(g >= heads)
    def _():
        for j in range(heads):
            rest[:, j * size:(j + 1) * size] = fin[j]

    @pl.when(g < heads)
    def _():
        rest[...] = d_ref[rows(c * size, size), :]

    for s in range(0, PB, BLOCK):
        e = s + BLOCK
        x = mm(rest[:, s:e], invs[s // BLOCK], ((1,), (1,)))
        x_ref[:, s:e] = x
        if e < PB:
            rest[:, e:] = rest[:, e:] - mm(x, fact[s:e, e:], ((1,), (0,)))

    while events:
        events.pop(0)[1]()

    own = both(both(first, c == 0), zb < heads)

    @pl.when(own)
    def _():
        for j in range(wide):
            tin[j] = d_ref[rows(z * share, share), j * size:(j + 1) * size]

    @pl.when(jnp.logical_not(own))
    def _():
        for j in range(wide):
            remote(tin.at[j], tin.at[j], t_send.at[0, 0], t_recv.at[j], partner).wait_recv()

    folded = jnp.logical_or(c == 0, both(first, zb < heads))
    for j in range(wide):
        at = pl.ds(j * size, size)
        out_ref[:, at] = jnp.where(folded, 0.0, a_ref[rows(z * share, share), at]) + tin[j]

    holds = c == (r * nc + zb) // wide

    def n_copy(i):
        return remote(psum, nbuf.at[r * nd + z], n_send.at[i], n_recv.at[r * nd + z], device(i))

    @pl.when(holds)
    def _():
        trailing = out_ref[...]
        grow = r * tile_rows + z * share + lax.broadcasted_iota(jnp.int32, trailing.shape, 0)
        gcol = c * tile_cols + lax.broadcasted_iota(jnp.int32, trailing.shape, 1)
        squares = jnp.where(grow == gcol, trailing * trailing, 0.0)
        acc = squares.reshape(share // 8, 8, tile_cols).sum(0)
        acc = sum(acc[:, i:i + LANES] for i in range(0, tile_cols, LANES))
        psum[...] = acc
        nbuf[r * nd + z] = acc

        @pl.loop(1, devices)
        def _(i):
            n_copy(i).start()

    acc = jnp.zeros((8, LANES), F32)
    for j in range(nr * nd):
        jr, jz = j // nd, j % nd
        mine = both(holds, both(r == jr, z == jz))

        @pl.when(jnp.logical_not(mine))
        def _():
            remote(psum, nbuf.at[j], n_send.at[0], n_recv.at[j], partner).wait_recv()

        acc = acc + nbuf[j]
    n_ref[...] = jnp.sqrt(jnp.sum(acc, keepdims=True) / (tile_cols * nc))

    @pl.when(holds)
    def _():
        @pl.loop(1, devices)
        def _(i):
            n_copy(i).wait_send()

    folds(lambda copy: copy.wait_send())

    @pl.when(first)
    def _():
        for j in range(heads):
            pair_copy(j).wait_send()
        for k in range(steps):
            din_copy(k).wait_send()
            for m in range(nc):
                f_copy(k, m).wait_send()
                if m:
                    d_copy(k, m).wait_send()

            @pl.when(inner)
            def _():
                dout_copy(k).wait_send()

    @pl.when(second)
    def _():
        for j in range(nc):
            pair_copy(j).wait_send()

    for s in range(slots):
        @pl.when(valid[s])
        def _():
            for q in (2 * s, 2 * s + 1):
                in_copy(q).wait_send()

                @pl.when(inner)
                def _():
                    out_copy(q).wait_send()

        for way, (cond, src, spot, to) in enumerate(routes(s)):
            @pl.when(both(cond, jnp.logical_not(here_is(to))))
            def _():
                remote(src, tin.at[spot], t_send.at[s, way], t_recv.at[spot], to).wait_send()


def local(sizes, a_tile, panels):
    nr, nc, nd = sizes
    tile_rows, tile_cols = a_tile.shape
    k_size = panels.shape[1]
    share, size = tile_rows // nd, tile_rows // nc
    heads, wide, steps, sub = PB // size, tile_cols // size, PB // BLOCK, BLOCK // nc
    lists = plan(nr, nc, heads)
    slots = max(map(len, lists))
    vmem = pl.BlockSpec(memory_space=pltpu.VMEM)
    shape = lambda *s: jax.ShapeDtypeStruct(s, F32)
    buf = lambda *s: pltpu.VMEM(s, F32)
    dma = lambda *s: pltpu.SemaphoreType.DMA(s)
    trailing, new_panel, norm = pl.pallas_call(
        functools.partial(kernel, sizes, lists),
        out_shape=(shape(share, tile_cols), shape(size, PB), shape(1, 1)),
        in_specs=[vmem] * 2,
        out_specs=(vmem,) * 3,
        scratch_shapes=[
            pltpu.VMEM((nr * tile_rows, k_size), BF16), pltpu.VMEM((nr * tile_rows, k_size), BF16),
            buf(nc, size, k_size), buf(slots, size, size), buf(2, slots, size, size), buf(slots, size, size),
            buf(slots, size, size), buf(wide, share, size),
            buf(BLOCK, PB), buf(2, BLOCK, PB), buf(PB, PB), buf(BLOCK, PB), buf(2 * heads, size // 2, size),
            buf(8, LANES), buf(nr * nd, 8, LANES),
            buf(BLOCK, 2 * BLOCK), buf(steps, BLOCK, BLOCK), buf(PB, PB), buf(size, PB),
            dma(nc), dma(nc), dma(steps, nc), dma(steps), dma(2 * heads, nc), dma(2 * heads),
            dma(2 * slots), dma(2, 2 * slots), dma(2 * slots), dma(2 * slots),
            dma(steps), dma(2, steps), dma(steps), dma(steps), dma(steps, nc), dma(steps, nc),
            dma(steps, nc), dma(steps, nc), dma(slots, 2), dma(wide), dma(nr * nc * nd), dma(nr * nd),
        ],
        compiler_params=pltpu.CompilerParams(collective_id=0, has_side_effects=True, vmem_limit_bytes=60 << 20),
        name="trailing_update",
    )(a_tile, panels)
    return (trailing, new_panel, norm.reshape(1))


def solution(mesh):
    sizes = tuple(mesh.shape[axis] for axis in ("row", "col", "depth"))
    return jax.shard_map(
        functools.partial(local, sizes),
        mesh=mesh,
        in_specs=(P("row", "col"), P("row", "depth")),
        out_specs=(P(("row", "depth"), "col"), P(("row", "col"), None), P()),
        check_vma=False,
    )
```

time: 107 us -> 79.2 us (0.74)
  Pallas kernels: 101 us -> 72.9 us
    pallas_call x1, Pallas kernels: 101 us -> 72.9 us  [local(): pl.pallas_call(functools.partial(kernel, sizes, lists), out_shape=(shape(...]
where the time goes in v1:
time: 79.2 us; the launch traced here: 78.9 us
  Pallas kernels  72.9 us (92%)
  local copies, waits for them, and re-layouts  3.74 us (5%)
  between operations  2.33 us (3%)
    pallas_call x1, Pallas kernels, local(): pl.pallas_call(functools.partial(kernel, sizes, lists), out_shape=(shape(...  72.9 us
    unnamed x2, local copies, waits for them, and re-layouts  3.74 us

profile of v1, /device:TPU:0, one launch (start us, length us, event | category | flops | bytes accessed | tf_op | source)
XLA Modules:
  0.0 78.9 jit_solution(1743543215770061733)
XLA Ops:
  0.6 72.9 %trailing_update.1 = (f32[256,512]{1,0:T(8,128)}, f32[256,512]{1,0:T(8,128)}, f32[1,1]{1,0:T(1,128)}) custom-call(f32[1024,512]{1,0:T(8,128)} %a_ref.1, f32[1024,1024]{1,0:T(8,128)} %p_ref.1), custom_call_target="tpu_custom_call" | custom-call | tf_op jit(solution)/shard_map/trailing_update/pallas_call | solution.py:588
  73.5 1.9 %copy.8 = f32[256,512]{1,0:T(8,128)} copy(f32[256,512]{1,0:T(8,128)} %get-tuple-element.12) | data formatting | bytes 1048576
  75.4 1.9 %copy.9 = f32[256,512]{1,0:T(8,128)} copy(f32[256,512]{1,0:T(8,128)} %get-tuple-element.13) | data formatting | bytes 1048576

commit v2 on v1

--- a/solution.py
+++ b/solution.py
@@ -12,7 +12,10 @@
 NB = 32
 LANES = 128
 TILE = 256
-EVENTS = {"open": 20.0, "tick": 1.15, "first": 13.0, "step": 2.8, "hop": 4.5}
+OPEN, TICK, HOP, NORM = 21.0, 1.05, 3.4, 37.0
+ARRIVALS = ((13.0, 1.6), (23.5, 1.5), (25.5, 1.4))
+EARLIEST = 17.5
+SENDS = ((0.0, 0.0), (19.5, 1.4), (21.0, 1.4))
 HIGHEST = lax.Precision.HIGHEST
 MESH = pl.DeviceIdType.MESH
 F32 = jnp.float32
@@ -67,7 +70,7 @@
 def plan(nr, nc, heads):
     lists = [[] for _ in range(nr * nc)]
     for g in range(heads, nr * nc):
-        lists[g] = [(g, j) for j in range(heads)] + [(g, g)]
+        lists[g] = [(g, g)] + [(g, j) for j in range(heads)]
     for low in range(heads, nr * nc):
         for high in range(low + 1, nr * nc):
             able = [g for g in range(nr * nc) if g < nc or g // nc == low // nc]
@@ -76,11 +79,11 @@
     return lists
 
 
-def kernel(sizes, lists, a_ref, p_ref, out_ref, x_ref, n_ref, *scratch):
+def kernel(sizes, lists, a_hbm, p_hbm, out_ref, x_ref, n_ref, *scratch):
     nr, nc, nd = sizes
-    (hi, lo, oth, part, rin, fin, turned, tin, dpart, drin, d_ref, adbuf, acbuf, psum, nbuf,
+    (a_ref, p_ref, hi, lo, oth, part, rin, fin, turned, tin, dpart, drin, d_ref, adbuf, acbuf, psum, nbuf,
      work, invs, fact, rest,
-     pair_send, pair_recv, ad_send, ad_recv, ac_send, ac_recv, in_send, in_recv, out_send, out_recv,
+     load, pair_send, pair_recv, ad_send, ad_recv, ac_send, ac_recv, in_send, in_recv, out_send, out_recv,
      di_send, di_recv, do_send, do_recv, d_send, d_recv, f_send, f_recv, t_send, t_recv, n_send, n_recv) = scratch
     tile_rows, tile_cols = a_ref.shape
     size = tile_rows // nc
@@ -128,6 +131,15 @@
     def rows(start, count):
         return pl.ds(pl.multiple_of(start, count), count)
 
+    def p_load(t):
+        at = pl.ds(t * TILE, TILE)
+        return pltpu.make_async_copy(p_hbm.at[at, :], p_ref.at[at, :], load.at[t])
+
+    a_load = pltpu.make_async_copy(a_hbm, a_ref, load.at[tile_rows // TILE])
+    for t in range(tile_rows // TILE):
+        p_load(t).start()
+    a_load.start()
+
     barrier = pltpu.get_barrier_semaphore()
     me = g * nd + z
 
@@ -135,16 +147,27 @@
         there = lax.rem(me + i, devices)
         return (there // (nc * nd), lax.rem(there // nd, nc), lax.rem(there, nd))
 
-    @pl.loop(1, devices)
-    def _(i):
-        pl.semaphore_signal(barrier, inc=1, device_id=device(i), device_id_type=MESH)
-
-    @pl.loop(0, tile_rows // TILE)
-    def _(t):
-        high, rem = split(p_ref[rows(t * TILE, TILE), :])
+    @pl.loop(0, nd)
+    def _(k):
+        depth = lax.rem(z + k, nd)
+        for i in range(nr * nc):
+            to = (r if i < nc else 1 - r, lax.rem(c + i % nc, nc), depth)
+            if i:
+                pl.semaphore_signal(barrier, inc=1, device_id=to, device_id_type=MESH)
+            else:
+                @pl.when(k > 0)
+                def _():
+                    pl.semaphore_signal(barrier, inc=1, device_id=to, device_id_type=MESH)
+
+    def split_own(t):
+        p_load(t).wait()
+        high, rem = split(p_ref[pl.ds(t * TILE, TILE), :])
         here = rows(r * tile_rows + t * TILE, TILE)
         hi[here, :] = high
         lo[here, :] = rem
+
+    for t in range(PB // TILE):
+        split_own(t)
 
     def compute(s):
         a, b = rows(xs[s] * size, size), rows(ys[s] * size, size)
@@ -157,6 +180,9 @@
         left_lo = jnp.concatenate([lo[i, :] for i in at], axis=0)
         dpart[...] = -product(left_hi, left_lo, hi[:PB, :], lo[:PB, :])
 
+    for t in range(PB // TILE, tile_rows // TILE):
+        split_own(t)
+    a_load.wait()
     for s in range(slots):
         pl.when(near[s])(functools.partial(compute, s))
 
@@ -181,36 +207,26 @@
         return remote(a_ref.at[d_at(to, k)], adbuf.at[d_in(k)], ad_send.at[k, to], ad_recv.at[k], (r, to, z))
 
     def ac_at(col, q):
-        return (rows(col * size + q % 2 * half, half), pl.ds(q // 2 * size, size))
+        return (rows(col * size + q % 2 * half, half), pl.ds((q // 2 - 1) * size, size))
 
     def ac_copy(q, to):
-        return remote(a_ref.at[ac_at(to, q)], acbuf.at[q], ac_send.at[q, to], ac_recv.at[q], (r, to, z))
-
-    @pl.when(first)
-    def _():
-        for j in range(heads):
-            pair_copy(j).start()
-
-    @pl.when(second)
-    def _():
-        for j in range(nc):
-            pair_copy(j).start()
-
-    def folds(act):
-        @pl.when(c == 0)
-        def _():
-            for k in range(steps):
-                @pl.when(both(first, z == d_fold(k)))
+        return remote(a_ref.at[ac_at(to, q)], acbuf.at[q - 2], ac_send.at[q - 2, to], ac_recv.at[q - 2], (r, to, z))
+
+    def d_folds(act):
+        for k in range(steps):
+            @pl.when(both(both(first, c == 0), z == d_fold(k)))
+            def _():
+                for to in range(1, nc):
+                    act(ad_copy(k, to))
+
+    def c_folds(act):
+        for q in range(2, 2 + 2 * heads):
+            for to in range(1, nc):
+                @pl.when(both(both(c == 0, z == c_fold(q)), r * nc + to >= heads))
                 def _():
-                    for to in range(1, nc):
-                        act(ad_copy(k, to))
-            for q in range(2 * heads):
-                for to in range(1, nc):
-                    @pl.when(both(z == c_fold(q), r * nc + to >= heads))
-                    def _():
-                        act(ac_copy(q, to))
-
-    folds(lambda copy: copy.start())
+                    act(ac_copy(q, to))
+
+    d_folds(lambda copy: copy.start())
 
     def din_copy(k):
         return remote(dpart.at[d_in(k)], drin.at[(side,) + d_in(k)], di_send.at[k], di_recv.at[side, k], (r, c, inward))
@@ -283,7 +299,7 @@
         def _():
             part[chunk(q)] = part[chunk(q)] + in_wait(0, q)[...]
 
-        if q < 2 * heads:
+        if 0 < q // 2 <= heads:
             @pl.when(both(g >= heads, z == c_fold(q)))
             def _():
                 @pl.when(c == 0)
@@ -293,7 +309,7 @@
                 @pl.when(c != 0)
                 def _():
                     ac_copy(q, 1).wait_recv()
-                    part[chunk(q)] = part[chunk(q)] + acbuf[q]
+                    part[chunk(q)] = part[chunk(q)] + acbuf[q - 2]
 
         in_copy(q).start()
 
@@ -324,8 +340,8 @@
                 def _():
                     remote(src, tin.at[spot], t_send.at[s, way], t_recv.at[spot], to).start()
 
-    def stage_b(q):
-        @pl.when(both(valid[q // 2], center))
+    def stage_b(q, member):
+        @pl.when(both(both(valid[q // 2], member), center))
         def _():
             fin[chunk(q)] = part[chunk(q)] + in_wait(1, q)[...]
 
@@ -336,8 +352,8 @@
             if q % 2:
                 deliver(q // 2)
 
-    def stage_c(q):
-        @pl.when(both(valid[q // 2], jnp.logical_not(center)))
+    def stage_c(q, member):
+        @pl.when(both(both(valid[q // 2], member), jnp.logical_not(center)))
         def _():
             out_copy(q).wait_recv()
 
@@ -348,8 +364,11 @@
             if q % 2:
                 deliver(q // 2)
 
-    def inner_a(q):
-        pl.when(both(valid[q // 2], inner))(functools.partial(stage_a, q))
+    def edge_send(q, member):
+        pl.when(both(both(valid[q // 2], member), edge))(functools.partial(stage_a, q))
+
+    def inner_a(q, member):
+        pl.when(both(both(valid[q // 2], member), inner))(functools.partial(stage_a, q))
 
     def edge_a(s, cond):
         @pl.when(both(edge, cond))
@@ -362,8 +381,18 @@
         for k in range(steps):
             stage_d(k)
 
-    for s in range(slots):
-        edge_a(s, both(first, near[s]))
+    @pl.when(first)
+    def _():
+        for j in range(heads):
+            pair_copy(j).start()
+
+    @pl.when(second)
+    def _():
+        for j in range(nc):
+            pair_copy(j).start()
+
+    c_folds(lambda copy: copy.start())
+    edge_a(0, both(second, near[0]))
 
     @pl.when(second)
     def _():
@@ -372,25 +401,94 @@
             high, rem = split(oth[j])
             hi[pl.ds(j * size, size), :] = high
             lo[pl.ds(j * size, size), :] = rem
-        for s in range(heads):
+        for s in range(1, 1 + heads):
             compute(s)
 
-    for s in range(slots):
+    for s in range(1, slots):
         edge_a(s, both(second, valid[s]))
+
+    def center_d(k):
+        @pl.when(center)
+        def _():
+            d_ref[d_at(c, k)] = dpart[d_in(k)] + din_wait(1, k)[...]
+            spread_d(k)
 
     @pl.when(both(first, inner))
     def _():
         for k in range(steps):
             stage_d(k)
-
-    def center_d(k):
-        d_ref[d_at(c, k)] = dpart[d_in(k)] + din_wait(1, k)[...]
-        spread_d(k)
-
-    @pl.when(both(first, center))
-    def _():
-        for k in range(steps):
-            center_d(k)
+            if k:
+                center_d(k - 1)
+        center_d(steps - 1)
+
+    def outer_d(k):
+        @pl.when(both(first, jnp.logical_not(center)))
+        def _():
+            dout_copy(k).wait_recv()
+            spread_d(k)
+
+    def gather_d(k):
+        @pl.when(first)
+        def _():
+            for m in range(1, nc):
+                d_from(k, m).wait_recv()
+                f_copy(k, m).start()
+
+    def arrive_d(k):
+        @pl.when(second)
+        def _():
+            for m in range(nc):
+                f_copy(k, m).wait_recv()
+
+    own = both(both(first, c == 0), zb < heads)
+    holds = c == (r * nc + zb) // wide
+    spot = lax.rem(r * nc + zb, wide)
+
+    def t_wait(j):
+        remote(tin.at[j], tin.at[j], t_send.at[0, 0], t_recv.at[j], partner).wait_recv()
+
+    def n_copy(i):
+        return remote(psum, nbuf.at[r * nd + z], n_send.at[i], n_recv.at[r * nd + z], device(i))
+
+    def norm_part():
+        for j in range(wide):
+            pl.when(both(both(holds, jnp.logical_not(own)), spot == j))(functools.partial(t_wait, j))
+
+        @pl.when(holds)
+        def _():
+            base = a_ref[rows(z * share, share), rows(spot * size, size)]
+            block = jnp.where(own, d_ref[rows(lax.rem(z * share, PB), share), rows(lax.rem(r * nc + zb, heads) * size, size)], base + tin[spot])
+            row = zo + lax.broadcasted_iota(jnp.int32, block.shape, 0)
+            squares = jnp.where(row == lax.broadcasted_iota(jnp.int32, block.shape, 1), block * block, 0.0)
+            acc = squares.reshape(share // 8, 8, size).sum(0)
+            acc = sum(acc[:, i:i + LANES] for i in range(0, size, LANES))
+            psum[...] = acc
+            nbuf[r * nd + z] = acc
+
+            @pl.loop(1, devices)
+            def _(i):
+                n_copy(i).start()
+
+    members = (second, both(first, g >= heads), g < heads)
+    events = []
+    for member, (arrive, step), (send, gap) in zip(members, ARRIVALS, SENDS):
+        for q in range(2 * slots):
+            for when, stage in enumerate((inner_a, stage_b, stage_c)):
+                events.append((arrive + step * q + when * HOP, q // 2 <= heads, functools.partial(stage, q, member)))
+            if send:
+                events.append((send + gap * q, q // 2 <= heads, functools.partial(edge_send, q, member)))
+    for k in range(1, steps):
+        events.append((OPEN + k, True, functools.partial(gather_d, k)))
+    events.append((NORM, False, norm_part))
+    events.sort(key=lambda e: e[0])
+
+    def advance(now):
+        while events and events[0][0] <= now:
+            events.pop(0)[2]()
+
+    advance(EARLIEST)
+    for k in range(steps):
+        outer_d(k)
 
     @pl.when(first)
     def _():
@@ -403,48 +501,22 @@
         for s in range(slots):
             pl.when(far[s])(functools.partial(compute, s))
 
-    for s in range(slots):
-        edge_a(s, both(first, far[s]))
-
-    times = EVENTS
-    events = []
-    for q in range(2 * slots):
-        t = times["first"] + times["step"] * q
-        events.append((t, functools.partial(inner_a, q)))
-        events.append((t + times["hop"], functools.partial(stage_b, q)))
-        events.append((t + 2 * times["hop"], functools.partial(stage_c, q)))
-    events.sort(key=lambda e: e[0])
-    clock = [times["open"]]
-
-    def advance(amount=0):
-        while events and events[0][0] <= clock[0]:
-            events.pop(0)[1]()
-        clock[0] += amount
-
-    @pl.when(both(first, jnp.logical_not(center)))
-    def _():
-        for k in range(steps):
-            dout_copy(k).wait_recv()
-            spread_d(k)
-
-    @pl.when(first)
-    def _():
-        for k in range(steps):
-            for m in range(1, nc):
-                d_from(k, m).wait_recv()
-                f_copy(k, m).start()
-
-    @pl.when(second)
-    def _():
-        for k in range(steps):
-            for m in range(nc):
-                f_copy(k, m).wait_recv()
+    gather_d(0)
+    arrive_d(0)
+    clock = [OPEN]
+
+    def tick():
+        advance(clock[0])
+        clock[0] += TICK
 
     for s in range(0, PB, BLOCK):
         e = s + BLOCK
         src = fact if s else d_ref
-        inv = factor_block(work, src[s:e, s:e], lambda: advance(times["tick"]))
+        inv = factor_block(work, src[s:e, s:e], tick)
         invs[s // BLOCK] = inv
+        if s == 0:
+            for k in range(1, steps):
+                arrive_d(k)
         if e < PB:
             u = mm(inv, src[s:e, e:], ((1,), (0,)))
             fact[s:e, e:] = u
@@ -458,13 +530,18 @@
                 d_ref[i * BLOCK:(i + 1) * BLOCK, j * BLOCK:(j + 1) * BLOCK] = (
                     d_ref[j * BLOCK:(j + 1) * BLOCK, i * BLOCK:(i + 1) * BLOCK].T)
 
-    while any(event.args[0] < 2 * heads for _, event in events):
-        events.pop(0)[1]()
+    @pl.when(own)
+    def _():
+        for j in range(wide):
+            tin[j] = d_ref[rows(z * share, share), j * size:(j + 1) * size]
+
+    while any(event[1] for event in events):
+        events.pop(0)[2]()
 
     @pl.when(g >= heads)
     def _():
         for j in range(heads):
-            rest[:, j * size:(j + 1) * size] = fin[j]
+            rest[:, j * size:(j + 1) * size] = fin[1 + j]
 
     @pl.when(g < heads)
     def _():
@@ -478,45 +555,18 @@
             rest[:, e:] = rest[:, e:] - mm(x, fact[s:e, e:], ((1,), (0,)))
 
     while events:
-        events.pop(0)[1]()
-
-    own = both(both(first, c == 0), zb < heads)
-
-    @pl.when(own)
+        events.pop(0)[2]()
+
+    @pl.when(jnp.logical_not(own))
     def _():
         for j in range(wide):
-            tin[j] = d_ref[rows(z * share, share), j * size:(j + 1) * size]
-
-    @pl.when(jnp.logical_not(own))
-    def _():
-        for j in range(wide):
-            remote(tin.at[j], tin.at[j], t_send.at[0, 0], t_recv.at[j], partner).wait_recv()
+            pl.when(jnp.logical_not(both(holds, spot == j)))(functools.partial(t_wait, j))
 
     folded = jnp.logical_or(c == 0, both(first, zb < heads))
     for j in range(wide):
         at = pl.ds(j * size, size)
         out_ref[:, at] = jnp.where(folded, 0.0, a_ref[rows(z * share, share), at]) + tin[j]
 
-    holds = c == (r * nc + zb) // wide
-
-    def n_copy(i):
-        return remote(psum, nbuf.at[r * nd + z], n_send.at[i], n_recv.at[r * nd + z], device(i))
-
-    @pl.when(holds)
-    def _():
-        trailing = out_ref[...]
-        grow = r * tile_rows + z * share + lax.broadcasted_iota(jnp.int32, trailing.shape, 0)
-        gcol = c * tile_cols + lax.broadcasted_iota(jnp.int32, trailing.shape, 1)
-        squares = jnp.where(grow == gcol, trailing * trailing, 0.0)
-        acc = squares.reshape(share // 8, 8, tile_cols).sum(0)
-        acc = sum(acc[:, i:i + LANES] for i in range(0, tile_cols, LANES))
-        psum[...] = acc
-        nbuf[r * nd + z] = acc
-
-        @pl.loop(1, devices)
-        def _(i):
-            n_copy(i).start()
-
     acc = jnp.zeros((8, LANES), F32)
     for j in range(nr * nd):
         jr, jz = j // nd, j % nd
@@ -535,7 +585,8 @@
         def _(i):
             n_copy(i).wait_send()
 
-    folds(lambda copy: copy.wait_send())
+    d_folds(lambda copy: copy.wait_send())
+    c_folds(lambda copy: copy.wait_send())
 
     @pl.when(first)
     def _():
@@ -582,27 +633,27 @@
     lists = plan(nr, nc, heads)
     slots = max(map(len, lists))
     vmem = pl.BlockSpec(memory_space=pltpu.VMEM)
-    shape = lambda *s: jax.ShapeDtypeStruct(s, F32)
     buf = lambda *s: pltpu.VMEM(s, F32)
     dma = lambda *s: pltpu.SemaphoreType.DMA(s)
     trailing, new_panel, norm = pl.pallas_call(
         functools.partial(kernel, sizes, lists),
-        out_shape=(shape(share, tile_cols), shape(size, PB), shape(1, 1)),
-        in_specs=[vmem] * 2,
+        out_shape=(buf(share, tile_cols), buf(size, PB), buf(1, 1)),
+        in_specs=[pl.BlockSpec(memory_space=pl.ANY)] * 2,
         out_specs=(vmem,) * 3,
         scratch_shapes=[
+            buf(tile_rows, tile_cols), buf(tile_rows, k_size),
             pltpu.VMEM((nr * tile_rows, k_size), BF16), pltpu.VMEM((nr * tile_rows, k_size), BF16),
             buf(nc, size, k_size), buf(slots, size, size), buf(2, slots, size, size), buf(slots, size, size),
             buf(slots, size, size), buf(wide, share, size),
             buf(BLOCK, PB), buf(2, BLOCK, PB), buf(PB, PB), buf(BLOCK, PB), buf(2 * heads, size // 2, size),
             buf(8, LANES), buf(nr * nd, 8, LANES),
             buf(BLOCK, 2 * BLOCK), buf(steps, BLOCK, BLOCK), buf(PB, PB), buf(size, PB),
-            dma(nc), dma(nc), dma(steps, nc), dma(steps), dma(2 * heads, nc), dma(2 * heads),
+            dma(tile_rows // TILE + 1), dma(nc), dma(nc), dma(steps, nc), dma(steps), dma(2 * heads, nc), dma(2 * heads),
             dma(2 * slots), dma(2, 2 * slots), dma(2 * slots), dma(2 * slots),
             dma(steps), dma(2, steps), dma(steps), dma(steps), dma(steps, nc), dma(steps, nc),
             dma(steps, nc), dma(steps, nc), dma(slots, 2), dma(wide), dma(nr * nc * nd), dma(nr * nd),
         ],
-        compiler_params=pltpu.CompilerParams(collective_id=0, has_side_effects=True, vmem_limit_bytes=60 << 20),
+        compiler_params=pltpu.CompilerParams(collective_id=0, has_side_effects=True, vmem_limit_bytes=62 << 20),
         name="trailing_update",
     )(a_tile, panels)
     return (trailing, new_panel, norm.reshape(1))

time: 79.2 us -> 59.8 us (0.76)
  the two profiles are of different devices: /device:TPU:0 before, /device:TPU:30 now
where the time goes in v2:
time: 59.8 us; the launch traced here: 59.6 us
  Pallas kernels  56.2 us (94%)
  between operations  1.8 us (3%)
  local copies, waits for them, and re-layouts  1.59 us (3%)
    pallas_call x1, Pallas kernels, local(): pl.pallas_call(functools.partial(kernel, sizes, lists), out_shape=(buf(sh...  56.2 us
    unnamed x2, local copies, waits for them, and re-layouts  1.59 us

profile of v2, /device:TPU:30, one launch (start us, length us, event | category | flops | bytes accessed | tf_op | source)
XLA Modules:
  0.0 59.6 jit_solution(2632375083772736485)
XLA Ops:
  0.6 56.2 %trailing_update.1 = (f32[256,512]{1,0:T(8,128)S(1)}, f32[256,512]{1,0:T(8,128)S(1)}, f32[1,1]{1,0:T(1,128)S(1)}) custom-call(f32[1024,512]{1,0:T(8,128)} %a_hbm.1, f32[1024,1024]{1,0:T(8,128)} %p_hbm.1), custom_call_target="tpu_custom_call" | custom-call | tf_op jit(solution)/shard_map/trailing_update/pallas_call | solution.py:638
  56.9 0.8 %copy.8 = f32[256,512]{1,0:T(8,128)} copy(f32[256,512]{1,0:T(8,128)S(1)} %get-tuple-element.9) | data formatting | bytes 1048576
  57.7 0.8 %copy.9 = f32[256,512]{1,0:T(8,128)} copy(f32[256,512]{1,0:T(8,128)S(1)} %get-tuple-element.10) | data formatting | bytes 1048576

commit v3 on v2

--- a/solution.py
+++ b/solution.py
@@ -12,11 +12,10 @@
 NB = 32
 LANES = 128
 TILE = 256
-OPEN, TICK, HOP, NORM = 21.0, 1.05, 3.4, 37.0
-ARRIVALS = ((13.0, 1.6), (23.5, 1.5), (25.5, 1.4))
-EARLIEST = 17.5
-SENDS = ((0.0, 0.0), (19.5, 1.4), (21.0, 1.4))
-HIGHEST = lax.Precision.HIGHEST
+OPEN, TICK, HOP, NORM = 19.5, 1.0, 3.4, 34.0
+ARRIVALS = ((12.5, 1.6), (23.0, 1.4), (23.0, 1.4))
+EARLIEST = 16.0
+SENDS = ((0.0, 0.0), (18.1, 1.4), (18.1, 1.4))
 MESH = pl.DeviceIdType.MESH
 F32 = jnp.float32
 BF16 = jnp.bfloat16
@@ -36,7 +35,10 @@
 
 
 def mm(a, b, dims):
-    return lax.dot_general(a, b, (dims, ((), ())), precision=HIGHEST, preferred_element_type=F32)
+    a_hi, a_lo = split(a)
+    b_hi, b_lo = split(b)
+    dot = lambda x, y: lax.dot_general(x, y, (dims, ((), ())), preferred_element_type=F32)
+    return dot(a_hi, b_hi) + (dot(a_hi, b_lo) + dot(a_lo, b_hi))
 
 
 def factor_block(work, block, advance):
@@ -81,7 +83,7 @@
 
 def kernel(sizes, lists, a_hbm, p_hbm, out_ref, x_ref, n_ref, *scratch):
     nr, nc, nd = sizes
-    (a_ref, p_ref, hi, lo, oth, part, rin, fin, turned, tin, dpart, drin, d_ref, adbuf, acbuf, psum, nbuf,
+    (a_ref, p_ref, hi, lo, oth, part, rin, fin, turned, tin, drin, d_ref, adbuf, acbuf, psum, nbuf, spent,
      work, invs, fact, rest,
      load, pair_send, pair_recv, ad_send, ad_recv, ac_send, ac_recv, in_send, in_recv, out_send, out_recv,
      di_send, di_recv, do_send, do_recv, d_send, d_recv, f_send, f_recv, t_send, t_recv, n_send, n_recv) = scratch
@@ -93,7 +95,8 @@
     share = tile_rows // nd
     sub = BLOCK // nc
     steps = PB // BLOCK
-    slots = max(map(len, lists))
+    slots, base = max(map(len, lists)), min(map(len, lists))
+    unit = sub * (steps + 1) // 2
     devices = nr * nc * nd
     r, c, z = lax.axis_index("row"), lax.axis_index("col"), lax.axis_index("depth")
     g = r * nc + c
@@ -178,7 +181,7 @@
         at = [pl.ds(pl.multiple_of(k * BLOCK + c * sub, sub), sub) for k in range(steps)]
         left_hi = jnp.concatenate([hi[i, :] for i in at], axis=0)
         left_lo = jnp.concatenate([lo[i, :] for i in at], axis=0)
-        dpart[...] = -product(left_hi, left_lo, hi[:PB, :], lo[:PB, :])
+        drin[z] = -product(left_hi, left_lo, hi[:PB, :], lo[:PB, :])
 
     for t in range(PB // TILE, tile_rows // TILE):
         split_own(t)
@@ -189,10 +192,13 @@
     pl.semaphore_wait(barrier, devices - 1)
 
     def pair_copy(j):
-        return remote(p_ref.at[rows(j * size, size), :], oth.at[j], pair_send.at[j], pair_recv.at[j], partner)
-
-    def d_fold(k):
-        return mid - 1 + k % 2
+        return remote(p_ref.at[rows(j * size, size), :], oth.at[j], pair_send, pair_recv, partner)
+
+    def pair_all(count):
+        return remote(oth.at[pl.ds(0, count)], oth.at[pl.ds(0, count)], pair_send, pair_recv, partner)
+
+    def rows_of(count):
+        return fact.at[pl.ds(0, count), :]
 
     def c_fold(q):
         return (mid - 1, mid, 0, nd - 1)[q % 4]
@@ -204,20 +210,19 @@
         return (pl.ds(k * sub, sub), pl.ds(k * BLOCK, PB - k * BLOCK))
 
     def ad_copy(k, to):
-        return remote(a_ref.at[d_at(to, k)], adbuf.at[d_in(k)], ad_send.at[k, to], ad_recv.at[k], (r, to, z))
+        return remote(a_ref.at[d_at(to, k)], adbuf.at[d_in(k)], ad_send, ad_recv.at[k], (r, to, z))
 
     def ac_at(col, q):
         return (rows(col * size + q % 2 * half, half), pl.ds((q // 2 - 1) * size, size))
 
     def ac_copy(q, to):
-        return remote(a_ref.at[ac_at(to, q)], acbuf.at[q - 2], ac_send.at[q - 2, to], ac_recv.at[q - 2], (r, to, z))
-
-    def d_folds(act):
+        return remote(a_ref.at[ac_at(to, q)], acbuf.at[q - 2], ac_send.at[(q - 2) // 2, to], ac_recv.at[q - 2], (r, to, z))
+
+    @pl.when(both(both(first, c == 0), center))
+    def _():
         for k in range(steps):
-            @pl.when(both(both(first, c == 0), z == d_fold(k)))
-            def _():
-                for to in range(1, nc):
-                    act(ad_copy(k, to))
+            for to in range(1, nc):
+                ad_copy(k, to).start()
 
     def c_folds(act):
         for q in range(2, 2 + 2 * heads):
@@ -226,55 +231,30 @@
                 def _():
                     act(ac_copy(q, to))
 
-    d_folds(lambda copy: copy.start())
-
-    def din_copy(k):
-        return remote(dpart.at[d_in(k)], drin.at[(side,) + d_in(k)], di_send.at[k], di_recv.at[side, k], (r, c, inward))
-
-    def din_wait(at, k):
-        here = drin.at[(at,) + d_in(k)]
-        remote(here, here, di_send.at[k], di_recv.at[at, k], (r, c, inward)).wait_recv()
-        return here
+    def din_copy(k, to):
+        here = drin.at[(z,) + d_in(k)]
+        return remote(here, here, di_send, di_recv.at[k], (r, c, to))
 
     def stage_d(k):
-        @pl.when(inner)
-        def _():
-            dpart[d_in(k)] = dpart[d_in(k)] + din_wait(0, k)[...]
-
-        @pl.when(z == d_fold(k))
-        def _():
-            @pl.when(c == 0)
-            def _():
-                dpart[d_in(k)] = dpart[d_in(k)] + a_ref[d_at(0, k)]
-
-            @pl.when(c != 0)
-            def _():
-                ad_copy(k, 1).wait_recv()
-                dpart[d_in(k)] = dpart[d_in(k)] + adbuf[d_in(k)]
-
-        din_copy(k).start()
-
-    def dout_copy(k):
+        for to in (mid - 1, mid):
+            pl.when(z != to)(din_copy(k, to).start)
+
+    def dout_copy(k, to):
         here = d_ref.at[d_at(c, k)]
-        return remote(here, here, do_send.at[k], do_recv.at[k], (r, c, outward))
+        return remote(here, here, do_send, do_recv.at[k], (r, c, to))
 
     def d_copy(k, m):
         here = d_ref.at[d_at(c, k)]
-        return remote(here, here, d_send.at[k, m], d_recv.at[k, m], (r, lax.rem(c + m, nc), z))
-
-    def d_from(k, m):
-        there = d_ref.at[d_at(lax.rem(c - m + nc, nc), k)]
-        return remote(there, there, d_send.at[k, m], d_recv.at[k, m], (r, lax.rem(c + m, nc), z))
+        return remote(here, here, d_send, d_recv.at[k], (r, lax.rem(c + m, nc), z))
+
+    def d_rows(k, count):
+        return d_ref.at[pl.ds(k * BLOCK, count), pl.ds(k * BLOCK, PB - k * BLOCK)]
 
     def f_copy(k, m):
         there = d_ref.at[d_at(lax.rem(c - m + nc, nc), k)]
-        return remote(there, there, f_send.at[k, m], f_recv.at[k, m], partner)
+        return remote(there, there, f_send, f_recv.at[k], partner)
 
     def spread_d(k):
-        @pl.when(inner)
-        def _():
-            dout_copy(k).start()
-
         for m in range(1, nc):
             d_copy(k, m).start()
         f_copy(k, 0).start()
@@ -283,16 +263,16 @@
         return (q // 2, pl.ds(q % 2 * half, half), slice(None))
 
     def in_copy(q):
-        return remote(part.at[chunk(q)], rin.at[(side,) + chunk(q)], in_send.at[q], in_recv.at[side, q], (r, c, inward))
+        return remote(part.at[chunk(q)], rin.at[(side,) + chunk(q)], in_send.at[max(0, q // 2 - base + 1)], in_recv.at[side, q], (r, c, inward))
 
     def in_wait(at, q):
         here = rin.at[(at,) + chunk(q)]
-        remote(here, here, in_send.at[q], in_recv.at[at, q], (r, c, inward)).wait_recv()
+        remote(here, here, in_send.at[0], in_recv.at[at, q], (r, c, inward)).wait_recv()
         return here
 
     def out_copy(q):
         here = fin.at[chunk(q)]
-        return remote(here, here, out_send.at[q], out_recv.at[q], (r, c, outward))
+        return remote(here, here, out_send.at[max(0, q // 2 - base + 1)], out_recv.at[q], (r, c, outward))
 
     def stage_a(q):
         @pl.when(inner)
@@ -376,7 +356,7 @@
             stage_a(2 * s)
             stage_a(2 * s + 1)
 
-    @pl.when(both(first, edge))
+    @pl.when(first)
     def _():
         for k in range(steps):
             stage_d(k)
@@ -396,8 +376,8 @@
 
     @pl.when(second)
     def _():
+        pair_all(heads).wait_recv()
         for j in range(heads):
-            pair_copy(j).wait_recv()
             high, rem = split(oth[j])
             hi[pl.ds(j * size, size), :] = high
             lo[pl.ds(j * size, size), :] = rem
@@ -408,37 +388,50 @@
         edge_a(s, both(second, valid[s]))
 
     def center_d(k):
-        @pl.when(center)
-        def _():
-            d_ref[d_at(c, k)] = dpart[d_in(k)] + din_wait(1, k)[...]
-            spread_d(k)
-
-    @pl.when(both(first, inner))
+        here = drin.at[(pl.ds(0, nd - 1),) + d_in(k)]
+        remote(here, here, di_send, di_recv.at[k], partner).wait_recv()
+        total = drin[(0,) + d_in(k)]
+        for j in range(1, nd):
+            total = total + drin[(j,) + d_in(k)]
+
+        @pl.when(c == 0)
+        def _():
+            d_ref[d_at(0, k)] = total + a_ref[d_at(0, k)]
+
+        @pl.when(c != 0)
+        def _():
+            ad_copy(k, 1).wait_recv()
+            d_ref[d_at(c, k)] = total + adbuf[d_in(k)]
+
+        for to in range(nd):
+            if to not in (mid - 1, mid):
+                pl.when(z == (mid - 1 if to < mid else mid))(dout_copy(k, to).start)
+        spread_d(k)
+
+    @pl.when(both(first, center))
     def _():
         for k in range(steps):
-            stage_d(k)
-            if k:
-                center_d(k - 1)
-        center_d(steps - 1)
+            center_d(k)
 
     def outer_d(k):
         @pl.when(both(first, jnp.logical_not(center)))
         def _():
-            dout_copy(k).wait_recv()
+            dout_copy(k, 0).wait_recv()
             spread_d(k)
 
     def gather_d(k):
         @pl.when(first)
         def _():
+            here = d_rows(k, BLOCK - sub)
+            remote(here, here, d_send, d_recv.at[k], partner).wait_recv()
             for m in range(1, nc):
-                d_from(k, m).wait_recv()
                 f_copy(k, m).start()
 
     def arrive_d(k):
         @pl.when(second)
         def _():
-            for m in range(nc):
-                f_copy(k, m).wait_recv()
+            here = d_rows(k, BLOCK)
+            remote(here, here, f_send, f_recv.at[k], partner).wait_recv()
 
     own = both(both(first, c == 0), zb < heads)
     holds = c == (r * nc + zb) // wide
@@ -448,7 +441,7 @@
         remote(tin.at[j], tin.at[j], t_send.at[0, 0], t_recv.at[j], partner).wait_recv()
 
     def n_copy(i):
-        return remote(psum, nbuf.at[r * nd + z], n_send.at[i], n_recv.at[r * nd + z], device(i))
+        return remote(psum, nbuf.at[r * nd + z], n_send, n_recv, device(i))
 
     def norm_part():
         for j in range(wide):
@@ -471,20 +464,34 @@
 
     members = (second, both(first, g >= heads), g < heads)
     events = []
-    for member, (arrive, step), (send, gap) in zip(members, ARRIVALS, SENDS):
-        for q in range(2 * slots):
+    for member, lists_of, (arrive, step), (send, gap) in zip(members, (lists[nc:], lists[heads:nc], lists[:heads]), ARRIVALS, SENDS):
+        for q in range(2 * max(map(len, lists_of))):
+            needed = q // 2 <= heads
             for when, stage in enumerate((inner_a, stage_b, stage_c)):
-                events.append((arrive + step * q + when * HOP, q // 2 <= heads, functools.partial(stage, q, member)))
+                events.append((arrive + step * q + when * HOP, needed, when == 2, functools.partial(stage, q, member)))
             if send:
-                events.append((send + gap * q, q // 2 <= heads, functools.partial(edge_send, q, member)))
+                events.append((send + gap * q, needed, True, functools.partial(edge_send, q, member)))
     for k in range(1, steps):
-        events.append((OPEN + k, True, functools.partial(gather_d, k)))
-    events.append((NORM, False, norm_part))
+        events.append((OPEN + k, True, None, functools.partial(gather_d, k)))
+    events.append((NORM, False, None, norm_part))
     events.sort(key=lambda e: e[0])
 
+    def run(batch):
+        for kind, cond in ((None, None), (False, inner), (True, jnp.logical_not(center))):
+            todo = [e[3] for e in batch if e[2] is kind]
+
+            def act():
+                for event in todo:
+                    event()
+
+            if todo:
+                act() if kind is None else pl.when(cond)(act)
+
     def advance(now):
+        batch = []
         while events and events[0][0] <= now:
-            events.pop(0)[2]()
+            batch.append(events.pop(0))
+        run(batch)
 
     advance(EARLIEST)
     for k in range(steps):
@@ -492,8 +499,8 @@
 
     @pl.when(first)
     def _():
+        pair_all(nc).wait_recv()
         for j in range(nc):
-            pair_copy(j).wait_recv()
             high, rem = split(oth[j])
             here = pl.ds(tile_rows + j * size, size)
             hi[here, :] = high
@@ -535,8 +542,9 @@
         for j in range(wide):
             tin[j] = d_ref[rows(z * share, share), j * size:(j + 1) * size]
 
-    while any(event[1] for event in events):
-        events.pop(0)[2]()
+    count = max([i + 1 for i, event in enumerate(events) if event[1]], default=0)
+    run(events[:count])
+    events = events[count:]
 
     @pl.when(g >= heads)
     def _():
@@ -554,8 +562,7 @@
         if e < PB:
             rest[:, e:] = rest[:, e:] - mm(x, fact[s:e, e:], ((1,), (0,)))
 
-    while events:
-        events.pop(0)[2]()
+    run(events)
 
     @pl.when(jnp.logical_not(own))
     def _():
@@ -567,57 +574,59 @@
         at = pl.ds(j * size, size)
         out_ref[:, at] = jnp.where(folded, 0.0, a_ref[rows(z * share, share), at]) + tin[j]
 
+    for count, cond in ((nr * nd - 1, holds), (nr * nd, jnp.logical_not(holds))):
+        here = nbuf.at[pl.ds(0, count)]
+        pl.when(cond)(remote(here, here, n_send, n_recv, partner).wait_recv)
     acc = jnp.zeros((8, LANES), F32)
     for j in range(nr * nd):
-        jr, jz = j // nd, j % nd
-        mine = both(holds, both(r == jr, z == jz))
-
-        @pl.when(jnp.logical_not(mine))
-        def _():
-            remote(psum, nbuf.at[j], n_send.at[0], n_recv.at[j], partner).wait_recv()
-
         acc = acc + nbuf[j]
     n_ref[...] = jnp.sqrt(jnp.sum(acc, keepdims=True) / (tile_cols * nc))
 
+    def sent(ref, sem):
+        remote(ref, ref, sem, n_recv, partner).wait_send()
+
     @pl.when(holds)
     def _():
-        @pl.loop(1, devices)
-        def _(i):
-            n_copy(i).wait_send()
-
-    d_folds(lambda copy: copy.wait_send())
+        sent(spent, n_send)
+
     c_folds(lambda copy: copy.wait_send())
 
     @pl.when(first)
     def _():
-        for j in range(heads):
-            pair_copy(j).wait_send()
-        for k in range(steps):
-            din_copy(k).wait_send()
-            for m in range(nc):
-                f_copy(k, m).wait_send()
-                if m:
-                    d_copy(k, m).wait_send()
-
-            @pl.when(inner)
+        pair_all(heads).wait_send()
+        sent(rows_of(nc * unit), f_send)
+        sent(rows_of((nc - 1) * unit), d_send)
+
+        @pl.when(center)
+        def _():
+            sent(rows_of(unit), di_send)
+            for _ in range(mid - 1):
+                sent(rows_of(unit), do_send)
+
+            @pl.when(c == 0)
             def _():
-                dout_copy(k).wait_send()
+                sent(rows_of((nc - 1) * unit), ad_send)
+
+        @pl.when(jnp.logical_not(center))
+        def _():
+            sent(rows_of(2 * unit), di_send)
 
     @pl.when(second)
     def _():
-        for j in range(nc):
-            pair_copy(j).wait_send()
+        pair_all(nc).wait_send()
+
+    def slots_sent(s, count, index):
+        sent(part.at[pl.ds(s, count)], in_send.at[index])
+
+        @pl.when(inner)
+        def _():
+            sent(fin.at[pl.ds(s, count)], out_send.at[index])
+
+    slots_sent(0, base, 0)
+    for s in range(base, slots):
+        pl.when(valid[s])(functools.partial(slots_sent, s, 1, s - base + 1))
 
     for s in range(slots):
-        @pl.when(valid[s])
-        def _():
-            for q in (2 * s, 2 * s + 1):
-                in_copy(q).wait_send()
-
-                @pl.when(inner)
-                def _():
-                    out_copy(q).wait_send()
-
         for way, (cond, src, spot, to) in enumerate(routes(s)):
             @pl.when(both(cond, jnp.logical_not(here_is(to))))
             def _():
@@ -631,7 +640,8 @@
     share, size = tile_rows // nd, tile_rows // nc
     heads, wide, steps, sub = PB // size, tile_cols // size, PB // BLOCK, BLOCK // nc
     lists = plan(nr, nc, heads)
-    slots = max(map(len, lists))
+    slots, base = max(map(len, lists)), min(map(len, lists))
+    one = pltpu.SemaphoreType.DMA
     vmem = pl.BlockSpec(memory_space=pltpu.VMEM)
     buf = lambda *s: pltpu.VMEM(s, F32)
     dma = lambda *s: pltpu.SemaphoreType.DMA(s)
@@ -645,13 +655,12 @@
             pltpu.VMEM((nr * tile_rows, k_size), BF16), pltpu.VMEM((nr * tile_rows, k_size), BF16),
             buf(nc, size, k_size), buf(slots, size, size), buf(2, slots, size, size), buf(slots, size, size),
             buf(slots, size, size), buf(wide, share, size),
-            buf(BLOCK, PB), buf(2, BLOCK, PB), buf(PB, PB), buf(BLOCK, PB), buf(2 * heads, size // 2, size),
-            buf(8, LANES), buf(nr * nd, 8, LANES),
+            buf(nd, BLOCK, PB), buf(PB, PB), buf(BLOCK, PB), buf(2 * heads, size // 2, size),
+            buf(8, LANES), buf(nr * nd, 8, LANES), buf(nr * nc * nd - 1, 8, LANES),
             buf(BLOCK, 2 * BLOCK), buf(steps, BLOCK, BLOCK), buf(PB, PB), buf(size, PB),
-            dma(tile_rows // TILE + 1), dma(nc), dma(nc), dma(steps, nc), dma(steps), dma(2 * heads, nc), dma(2 * heads),
-            dma(2 * slots), dma(2, 2 * slots), dma(2 * slots), dma(2 * slots),
-            dma(steps), dma(2, steps), dma(steps), dma(steps), dma(steps, nc), dma(steps, nc),
-            dma(steps, nc), dma(steps, nc), dma(slots, 2), dma(wide), dma(nr * nc * nd), dma(nr * nd),
+            dma(tile_rows // TILE + 1), one, one, one, dma(steps), dma(2, nc), dma(2 * heads),
+            dma(slots - base + 1), dma(2, 2 * slots), dma(slots - base + 1), dma(2 * slots),
+            one, dma(steps), one, dma(steps), one, dma(steps), one, dma(steps), dma(slots, 2), dma(wide), one, one,
         ],
         compiler_params=pltpu.CompilerParams(collective_id=0, has_side_effects=True, vmem_limit_bytes=62 << 20),
         name="trailing_update",

time: 59.8 us -> 56.3 us (0.941)
  Pallas kernels: 56.2 us -> 52.7 us
    pallas_call x1, Pallas kernels: 56.2 us -> 52.7 us  [local(): pl.pallas_call(functools.partial(kernel, sizes, lists), out_shape=(buf(sh...]
where the time goes in v3:
time: 56.3 us; the launch traced here: 56.1 us
  Pallas kernels  52.7 us (94%)
  between operations  1.8 us (3%)
  local copies, waits for them, and re-layouts  1.59 us (3%)
    pallas_call x1, Pallas kernels, local(): pl.pallas_call(functools.partial(kernel, sizes, lists), out_shape=(buf(sh...  52.7 us
    unnamed x2, local copies, waits for them, and re-layouts  1.59 us

profile of v3, /device:TPU:30, one launch (start us, length us, event | category | flops | bytes accessed | tf_op | source)
XLA Modules:
  0.0 56.1 jit_solution(4754404510218087775)
XLA Ops:
  0.6 52.7 %trailing_update.1 = (f32[256,512]{1,0:T(8,128)S(1)}, f32[256,512]{1,0:T(8,128)S(1)}, f32[1,1]{1,0:T(1,128)S(1)}) custom-call(f32[1024,512]{1,0:T(8,128)} %a_hbm.1, f32[1024,1024]{1,0:T(8,128)} %p_hbm.1), custom_call_target="tpu_custom_call" | custom-call | tf_op jit(solution)/shard_map/trailing_update/pallas_call | solution.py:648
  53.4 0.8 %copy.8 = f32[256,512]{1,0:T(8,128)} copy(f32[256,512]{1,0:T(8,128)S(1)} %get-tuple-element.9) | data formatting | bytes 1048576
  54.2 0.8 %copy.9 = f32[256,512]{1,0:T(8,128)} copy(f32[256,512]{1,0:T(8,128)S(1)} %get-tuple-element.10) | data formatting | bytes 1048576

commit v4 on v3

--- a/solution.py
+++ b/solution.py
@@ -12,10 +12,10 @@
 NB = 32
 LANES = 128
 TILE = 256
-OPEN, TICK, HOP, NORM = 19.5, 1.0, 3.4, 34.0
-ARRIVALS = ((12.5, 1.6), (23.0, 1.4), (23.0, 1.4))
-EARLIEST = 16.0
-SENDS = ((0.0, 0.0), (18.1, 1.4), (18.1, 1.4))
+OPEN, TICK, HOP, NORM = 18.0, 1.0, 4.3, 42.0
+ARRIVALS = ((13.5, 15.3, 18.0, 20.3, 22.6, 25.0, 27.5, 30.0, 32.5, 35.0), (24.5, 26.5, 29.0, 31.5, 33.8, 35.4, 37.0, 38.5))
+EARLIEST = 16.5
+SENDS = (16.5, 1.4)
 MESH = pl.DeviceIdType.MESH
 F32 = jnp.float32
 BF16 = jnp.bfloat16
@@ -69,15 +69,37 @@
     return work[:, BLOCK:]
 
 
-def plan(nr, nc, heads):
+def plan(nr, nc, heads, wide):
     lists = [[] for _ in range(nr * nc)]
+    pairs = [(high, low) for low in range(heads, nr * nc) for high in range(low + 1, nr * nc)]
     for g in range(heads, nr * nc):
         lists[g] = [(g, g)] + [(g, j) for j in range(heads)]
-    for low in range(heads, nr * nc):
-        for high in range(low + 1, nr * nc):
-            able = [g for g in range(nr * nc) if g < nc or g // nc == low // nc]
-            best = min(able, key=lambda g: (len(lists[g]), g not in (low, high), g))
-            lists[best].append((low, high) if best == low else (high, low))
+
+    def far(g, pair):
+        ends = [(x, y) for x, y in (pair, pair[::-1]) if x % nc in (0, nc - 1)]
+        return sum((x // nc) * nc + y // wide != g for x, y in ends)
+
+    late = {}
+    for near in (True, False):
+        for g in range(nc):
+            found = [p for p in pairs if p[1] < nc and not far(g, p) and any(b % nc in (0, nc - 1) for b in p) == near]
+            if g not in late and found:
+                late[g] = found[0]
+                pairs.remove(found[0])
+    for high, low in pairs:
+        able = [g for g in range(nr * nc) if g < nc or g // nc == low // nc]
+        best = min(able, key=lambda g: (len(lists[g]) + (g in late), g not in (low, high), g))
+        lists[best].append((high, low))
+    for g, pair in late.items():
+        lists[g].append(pair)
+    base = min(map(len, lists))
+    lists = [[pair + (3,) for pair in l] for l in lists]
+    for g, l in enumerate(lists):
+        for x, y, part in l[base:]:
+            able = [h for h in range(nr * nc) if h % nc != g % nc and len(lists[h]) == base and (h < nc or h // nc == min(x, y) // nc)]
+            if part == 3 and able:
+                l[l.index((x, y, part))] = (x, y, 1)
+                lists[able[-1]].append((x, y, 2))
     return lists
 
 
@@ -123,7 +145,9 @@
     xs = [pick([l[s][0] if s < len(l) else 0 for l in lists]) for s in range(slots)]
     ys = [pick([l[s][1] if s < len(l) else 0 for l in lists]) for s in range(slots)]
     counts = pick([len(l) for l in lists])
+    masks = [pick([l[s][2] if s < len(l) else 0 for l in lists]) for s in range(slots)]
     valid = [s < counts for s in range(slots)]
+    live = [both(valid[q // 2], masks[q // 2] != 2 - q % 2) for q in range(2 * slots)]
     near = [both(valid[s], both(xs[s] // nc == r, ys[s] // nc == r)) for s in range(slots)]
     far = [both(valid[s], jnp.logical_not(both(xs[s] // nc == r, ys[s] // nc == r))) for s in range(slots)]
 
@@ -192,10 +216,10 @@
     pl.semaphore_wait(barrier, devices - 1)
 
     def pair_copy(j):
-        return remote(p_ref.at[rows(j * size, size), :], oth.at[j], pair_send, pair_recv, partner)
+        return remote(p_ref.at[rows(j * size, size), :], oth.at[j], pair_send, pair_recv.at[j], partner)
 
     def pair_all(count):
-        return remote(oth.at[pl.ds(0, count)], oth.at[pl.ds(0, count)], pair_send, pair_recv, partner)
+        return remote(oth.at[pl.ds(0, count)], oth.at[pl.ds(0, count)], pair_send, pair_recv.at[0], partner)
 
     def rows_of(count):
         return fact.at[pl.ds(0, count), :]
@@ -263,7 +287,7 @@
         return (q // 2, pl.ds(q % 2 * half, half), slice(None))
 
     def in_copy(q):
-        return remote(part.at[chunk(q)], rin.at[(side,) + chunk(q)], in_send.at[max(0, q // 2 - base + 1)], in_recv.at[side, q], (r, c, inward))
+        return remote(part.at[chunk(q)], rin.at[(side,) + chunk(q)], in_send.at[max(0, q - 2 * base + 1)], in_recv.at[side, q], (r, c, inward))
 
     def in_wait(at, q):
         here = rin.at[(at,) + chunk(q)]
@@ -272,7 +296,7 @@
 
     def out_copy(q):
         here = fin.at[chunk(q)]
-        return remote(here, here, out_send.at[max(0, q // 2 - base + 1)], out_recv.at[q], (r, c, outward))
+        return remote(here, here, out_send.at[q], out_recv.at[q], (r, c, outward))
 
     def stage_a(q):
         @pl.when(inner)
@@ -293,68 +317,85 @@
 
         in_copy(q).start()
 
+    def wanted(s, plane):
+        last = plane * share // size
+        reaches = lambda block: jnp.where(low, lax.rem(block, nc) <= last, lax.rem(block, nc) >= last)
+        needed = jnp.logical_or(reaches(xs[s]), reaches(ys[s]))
+        return jnp.logical_or(needed, g >= heads) if 0 < s <= heads else needed
+
+    outgoing = [both(both(live[q], inner), wanted(q // 2, outward)) for q in range(2 * slots)]
+    incoming = [both(both(live[q], jnp.logical_not(center)), wanted(q // 2, z)) for q in range(2 * slots)]
+
     def here_is(device):
         return both(device[0] == r, device[1] == c)
 
-    def routes(s):
+    def routes(q):
+        s, h = q // 2, q % 2
         x, y = xs[s], ys[s]
         straight = (x // nc, y // wide, z)
         across = (y // nc, x // wide, z)
-        return (
-            (both(valid[s], zb == lax.rem(x, nc)), fin.at[s, rows(zo, share), :], lax.rem(y, wide), straight),
-            (both(both(valid[s], x != y), zb == lax.rem(y, nc)), turned.at[s, rows(zo, share), :], lax.rem(x, wide), across),
-        )
-
-    def deliver(s):
-        for way, (cond, src, spot, to) in enumerate(routes(s)):
+        found = []
+        for e in range(1 if share == size else 2):
+            cond = both(live[q], zb == lax.rem(x, nc))
+            if share == size:
+                cut, e = (pl.ds(h * half, half), slice(None)), h
+                src = fin.at[(s,) + cut]
+            else:
+                cond = both(cond, zo // half == h)
+                cut = (slice(None), pl.ds(e * half, half))
+                src = fin.at[s, rows(zo, share), pl.ds(e * half, half)]
+            found.append((cond, src, lax.rem(y, wide), cut, e, straight))
+        cut = (slice(None), pl.ds(h * half, half))
+        found.append((both(both(live[q], x != y), zb == lax.rem(y, nc)),
+                      turned.at[s, rows(zo, share), pl.ds(h * half, half)], lax.rem(x, wide), cut, h, across))
+        return found
+
+    def route_copy(q, way):
+        _, src, spot, cut, e, to = routes(q)[way]
+        return remote(src, tin.at[(spot,) + cut], t_send.at[q, way], t_recv.at[spot, e], to)
+
+    def deliver(q):
+        found = routes(q)
+        for way, (cond, src, spot, cut, e, to) in enumerate(found):
             @pl.when(cond)
             def _():
-                if way:
-                    turned[s] = fin[s].T
+                if way == len(found) - 1:
+                    turned[q // 2, :, pl.ds(q % 2 * half, half)] = fin[chunk(q)].T
 
                 @pl.when(here_is(to))
                 def _():
-                    pltpu.make_async_copy(src, tin.at[spot], t_recv.at[spot]).start()
-
-                @pl.when(jnp.logical_not(here_is(to)))
-                def _():
-                    remote(src, tin.at[spot], t_send.at[s, way], t_recv.at[spot], to).start()
+                    pltpu.make_async_copy(src, tin.at[(spot,) + cut], t_recv.at[spot, e]).start()
+
+                pl.when(jnp.logical_not(here_is(to)))(route_copy(q, way).start)
 
     def stage_b(q, member):
-        @pl.when(both(both(valid[q // 2], member), center))
+        @pl.when(both(both(live[q], member), center))
         def _():
             fin[chunk(q)] = part[chunk(q)] + in_wait(1, q)[...]
-
-            @pl.when(inner)
-            def _():
-                out_copy(q).start()
-
-            if q % 2:
-                deliver(q // 2)
+            pl.when(outgoing[q])(out_copy(q).start)
+            deliver(q)
 
     def stage_c(q, member):
-        @pl.when(both(both(valid[q // 2], member), jnp.logical_not(center)))
+        @pl.when(both(member, incoming[q]))
         def _():
             out_copy(q).wait_recv()
-
-            @pl.when(inner)
-            def _():
-                out_copy(q).start()
-
-            if q % 2:
-                deliver(q // 2)
+            pl.when(outgoing[q])(out_copy(q).start)
+            deliver(q)
 
     def edge_send(q, member):
-        pl.when(both(both(valid[q // 2], member), edge))(functools.partial(stage_a, q))
+        pl.when(both(both(live[q], member), edge))(functools.partial(stage_a, q))
 
     def inner_a(q, member):
-        pl.when(both(both(valid[q // 2], member), inner))(functools.partial(stage_a, q))
+        pl.when(both(both(live[q], member), inner))(functools.partial(stage_a, q))
 
     def edge_a(s, cond):
         @pl.when(both(edge, cond))
         def _():
-            stage_a(2 * s)
-            stage_a(2 * s + 1)
+            for q in (2 * s, 2 * s + 1):
+                if s < base:
+                    stage_a(q)
+                else:
+                    pl.when(live[q])(functools.partial(stage_a, q))
 
     @pl.when(first)
     def _():
@@ -372,20 +413,30 @@
             pair_copy(j).start()
 
     c_folds(lambda copy: copy.start())
-    edge_a(0, both(second, near[0]))
+    def split_pair(j, at):
+        pair_copy(j).wait_recv()
+        high, rem = split(oth[j])
+        hi[pl.ds(at, size), :] = high
+        lo[pl.ds(at, size), :] = rem
 
     @pl.when(second)
     def _():
-        pair_all(heads).wait_recv()
         for j in range(heads):
-            high, rem = split(oth[j])
-            hi[pl.ds(j * size, size), :] = high
-            lo[pl.ds(j * size, size), :] = rem
-        for s in range(1, 1 + heads):
-            compute(s)
+            split_pair(j, j * size)
+            compute(1 + j)
+            if j == 0:
+                edge_a(0, near[0])
 
     for s in range(1, slots):
         edge_a(s, both(second, valid[s]))
+
+    def far_part(j):
+        @pl.when(first)
+        def _():
+            split_pair(j, tile_rows + j * size)
+            for s in range(slots):
+                latest = jnp.maximum(xs[s], ys[s])
+                pl.when(both(far[s], latest == nc + j))(functools.partial(compute, s))
 
     def center_d(k):
         here = drin.at[(pl.ds(0, nd - 1),) + d_in(k)]
@@ -438,7 +489,10 @@
     spot = lax.rem(r * nc + zb, wide)
 
     def t_wait(j):
-        remote(tin.at[j], tin.at[j], t_send.at[0, 0], t_recv.at[j], partner).wait_recv()
+        for h in range(2):
+            at = pl.ds(h * half, half)
+            here = tin.at[j, at, :] if share == size else tin.at[j, :, at]
+            remote(here, here, n_send, t_recv.at[j, h], partner).wait_recv()
 
     def n_copy(i):
         return remote(psum, nbuf.at[r * nd + z], n_send, n_recv, device(i))
@@ -464,13 +518,15 @@
 
     members = (second, both(first, g >= heads), g < heads)
     events = []
-    for member, lists_of, (arrive, step), (send, gap) in zip(members, (lists[nc:], lists[heads:nc], lists[:heads]), ARRIVALS, SENDS):
+    for group, (member, lists_of) in enumerate(zip(members, (lists[nc:], lists[heads:nc], lists[:heads]))):
+        arrivals = ARRIVALS[min(group, 1)]
         for q in range(2 * max(map(len, lists_of))):
             needed = q // 2 <= heads
+            arrive = arrivals[min(q, len(arrivals) - 1)]
             for when, stage in enumerate((inner_a, stage_b, stage_c)):
-                events.append((arrive + step * q + when * HOP, needed, when == 2, functools.partial(stage, q, member)))
-            if send:
-                events.append((send + gap * q, needed, True, functools.partial(edge_send, q, member)))
+                events.append((arrive + when * HOP, needed, when == 2, functools.partial(stage, q, member)))
+            if group:
+                events.append((SENDS[0] + SENDS[1] * q, needed, True, functools.partial(edge_send, q, member)))
     for k in range(1, steps):
         events.append((OPEN + k, True, None, functools.partial(gather_d, k)))
     events.append((NORM, False, None, norm_part))
@@ -493,20 +549,15 @@
             batch.append(events.pop(0))
         run(batch)
 
+    early = nc - 1
+    for j in range(early):
+        far_part(j)
     advance(EARLIEST)
     for k in range(steps):
         outer_d(k)
 
-    @pl.when(first)
-    def _():
-        pair_all(nc).wait_recv()
-        for j in range(nc):
-            high, rem = split(oth[j])
-            here = pl.ds(tile_rows + j * size, size)
-            hi[here, :] = high
-            lo[here, :] = rem
-        for s in range(slots):
-            pl.when(far[s])(functools.partial(compute, s))
+    for j in range(early, nc):
+        far_part(j)
 
     gather_d(0)
     arrive_d(0)
@@ -618,19 +669,13 @@
     def slots_sent(s, count, index):
         sent(part.at[pl.ds(s, count)], in_send.at[index])
 
-        @pl.when(inner)
-        def _():
-            sent(fin.at[pl.ds(s, count)], out_send.at[index])
-
     slots_sent(0, base, 0)
-    for s in range(base, slots):
-        pl.when(valid[s])(functools.partial(slots_sent, s, 1, s - base + 1))
-
-    for s in range(slots):
-        for way, (cond, src, spot, to) in enumerate(routes(s)):
-            @pl.when(both(cond, jnp.logical_not(here_is(to))))
-            def _():
-                remote(src, tin.at[spot], t_send.at[s, way], t_recv.at[spot], to).wait_send()
+    for q in range(2 * base, 2 * slots):
+        pl.when(live[q])(functools.partial(sent, part.at[chunk(q)], in_send.at[q - 2 * base + 1]))
+    for q in range(2 * slots):
+        pl.when(outgoing[q])(functools.partial(sent, fin.at[chunk(q)], out_send.at[q]))
+        for way, (cond, _, _, _, _, to) in enumerate(routes(q)):
+            pl.when(both(cond, jnp.logical_not(here_is(to))))(route_copy(q, way).wait_send)
 
 
 def local(sizes, a_tile, panels):
@@ -639,7 +684,7 @@
     k_size = panels.shape[1]
     share, size = tile_rows // nd, tile_rows // nc
     heads, wide, steps, sub = PB // size, tile_cols // size, PB // BLOCK, BLOCK // nc
-    lists = plan(nr, nc, heads)
+    lists = plan(nr, nc, heads, wide)
     slots, base = max(map(len, lists)), min(map(len, lists))
     one = pltpu.SemaphoreType.DMA
     vmem = pl.BlockSpec(memory_space=pltpu.VMEM)
@@ -658,9 +703,9 @@
             buf(nd, BLOCK, PB), buf(PB, PB), buf(BLOCK, PB), buf(2 * heads, size // 2, size),
             buf(8, LANES), buf(nr * nd, 8, LANES), buf(nr * nc * nd - 1, 8, LANES),
             buf(BLOCK, 2 * BLOCK), buf(steps, BLOCK, BLOCK), buf(PB, PB), buf(size, PB),
-            dma(tile_rows // TILE + 1), one, one, one, dma(steps), dma(2, nc), dma(2 * heads),
-            dma(slots - base + 1), dma(2, 2 * slots), dma(slots - base + 1), dma(2 * slots),
-            one, dma(steps), one, dma(steps), one, dma(steps), one, dma(steps), dma(slots, 2), dma(wide), one, one,
+            dma(tile_rows // TILE + 1), one, dma(nc), one, dma(steps), dma(2, nc), dma(2 * heads),
+            dma(2 * (slots - base) + 1), dma(2, 2 * slots), dma(2 * slots), dma(2 * slots),
+            one, dma(steps), one, dma(steps), one, dma(steps), one, dma(steps), dma(2 * slots, 2 if share == size else 3), dma(wide, 2), one, one,
         ],
         compiler_params=pltpu.CompilerParams(collective_id=0, has_side_effects=True, vmem_limit_bytes=62 << 20),
         name="trailing_update",

time: 56.3 us -> 54.4 us (0.966)
  Pallas kernels: 52.7 us -> 50.3 us
    pallas_call x1, Pallas kernels: 52.7 us -> 50.3 us  [local(): pl.pallas_call(functools.partial(kernel, sizes, lists), out_shape=(buf(sh...]
where the time goes in v4:
time: 54.4 us; the launch traced here: 53.7 us
  Pallas kernels  50.3 us (92%)
  between operations  1.8 us (3%)
  local copies, waits for them, and re-layouts  1.59 us (3%)
    pallas_call x1, Pallas kernels, local(): pl.pallas_call(functools.partial(kernel, sizes, lists), out_shape=(buf(sh...  50.3 us
    unnamed x2, local copies, waits for them, and re-layouts  1.59 us

profile of v4, /device:TPU:30, one launch (start us, length us, event | category | flops | bytes accessed | tf_op | source)
XLA Modules:
  0.0 53.7 jit_solution(7903387771944657244)
XLA Ops:
  0.6 50.3 %trailing_update.1 = (f32[256,512]{1,0:T(8,128)S(1)}, f32[256,512]{1,0:T(8,128)S(1)}, f32[1,1]{1,0:T(1,128)S(1)}) custom-call(f32[1024,512]{1,0:T(8,128)} %a_hbm.1, f32[1024,1024]{1,0:T(8,128)} %p_hbm.1), custom_call_target="tpu_custom_call" | custom-call | tf_op jit(solution)/shard_map/trailing_update/pallas_call | solution.py:693
  51.0 0.8 %copy.8 = f32[256,512]{1,0:T(8,128)} copy(f32[256,512]{1,0:T(8,128)S(1)} %get-tuple-element.9) | data formatting | bytes 1048576
  51.8 0.8 %copy.9 = f32[256,512]{1,0:T(8,128)} copy(f32[256,512]{1,0:T(8,128)S(1)} %get-tuple-element.10) | data formatting | bytes 1048576
